TPU v7x, 128 devices: a whole 4x4x4 slice. The times are simulated.
128 devices in a mesh: datb: 4 (over z), model: 4 (over y), data: 8 (over x, core).
Axes of the slice: x: 4, y: 4, z: 4, core: 2. Of those that a mesh axis runs over, the one named last changes fastest.
Arguments:
- tokens: bfloat16 [8192, 3584], P(('datb', 'data', 'model'))
- w_gate: bfloat16 [3584, 18944], P(('datb', 'data'), 'model')
- w_up: bfloat16 [3584, 18944], P(('datb', 'data'), 'model')
- w_down: bfloat16 [18944, 3584], P('model', ('datb', 'data'))
- grad_out: bfloat16 [8192, 3584], P(('datb', 'data', 'model'))
Outputs:
- output 1: bfloat16 [8192, 3584], P(('datb', 'data', 'model'))
- output 2: bfloat16 [8192, 3584], P(('datb', 'data', 'model'))
- output 3: float32 [3584, 18944], P(('datb', 'data'), 'model')
- output 4: float32 [3584, 18944], P(('datb', 'data'), 'model')
- output 5: float32 [18944, 3584], P('model', ('datb', 'data'))
All inputs are finite; a program needn't handle non-finite values.
Results may differ from a plain program's by a relative error of at most 0.02.
Values are sent between devices in bfloat16 or wider.
A program may use at most 1 GiB of HBM per device.

v0:
```python
import functools

import jax
import jax.numpy as jnp
from jax import lax
from jax.experimental import pallas as pl
from jax.experimental.pallas import tpu as pltpu
from jax.sharding import Mesh
from jax.sharding import PartitionSpec as P

ROW_SPEC = P(("datb", "x", "core", "model"), None)
GATE_SPEC = P(("datb", "x", "core"), "model")
DOWN_SPEC = P("model", ("datb", "x", "core"))
BF16 = jnp.bfloat16
F32 = jnp.float32
MESH_ID = pl.DeviceIdType.MESH
RING = 4
NEAR = ((0, 0), (0, 1), (1, 0), (3, 0), (1, 1), (3, 1), (2, 0), (2, 1))
DELTAS = (0, 3, 1, 2)


def dot(a, b, ca, cb):
    return lax.dot_general(a, b, (((ca,), (cb,)), ((), ())), preferred_element_type=F32)


def gather_kernel(pg, pu, pd, tok, grad, wg, wu, wd, tok_all, grad_all,
                  own_sem, ex_s, ex_r, z1_s, z1_r, z2_s, z2_r, p1_s, p1_r, p2_s, p2_r, q1_s, q1_r, q2_s, q2_r, cc_s, cc_r):
    z, y = lax.axis_index("datb"), lax.axis_index("model")
    x, core = lax.axis_index("x"), lax.axis_index("core")
    i8 = 2 * x + core
    n8 = 2 * RING
    rows = tok.shape[0]
    half = rows // 2

    def peer(dx, dc):
        return 2 * lax.rem(x + dx, RING) + lax.rem(core + dc, 2)

    def zdev(k):
        return {"datb": lax.rem(z + k, RING)}

    def near(dx, dc):
        return {"x": lax.rem(x + dx, RING), "core": lax.rem(core + dc, 2)}

    def xdev(k):
        return {"x": lax.rem(x + k, RING)}

    def ydev(k):
        return {"model": lax.rem(y + k, RING)}

    def copy(src, dst, s, r, dev):
        return pltpu.make_async_remote_copy(src_ref=src, dst_ref=dst, send_sem=s, recv_sem=r, device_id=dev, device_id_type=MESH_ID)

    barrier = pltpu.get_barrier_semaphore()
    others = [zdev(1), zdev(3), ydev(1), ydev(3)] + [near(*n) for n in NEAR[1:]]
    for dev in others:
        pl.semaphore_signal(barrier, inc=1, device_id=dev, device_id_type=MESH_ID)
    pl.semaphore_wait(barrier, len(others))

    pieces, fulls = (pg, pu, pd), (wg, wu, wd)
    started = []

    def go(c):
        c.start()
        started.append(c)
        return c

    local = []
    for t in range(3):
        local.append(pltpu.make_async_copy(pieces[t].at[i8], fulls[t].at[z * n8 + i8], own_sem.at[t]))
    rings = ((tok, tok_all), (grad, grad_all))

    def row_block(px, py, lo=0, size=rows):
        start = (lax.rem(px, RING) * 2 + core) * RING + lax.rem(py, RING)
        return pl.ds(pl.multiple_of(start * rows + lo, half), size)

    for t, (own, full) in enumerate(rings):
        local.append(pltpu.make_async_copy(own, full.at[row_block(x, y)], own_sem.at[3 + t]))
    for c in local:
        c.start()

    def exchange(t):
        for k in range(1, n8):
            go(copy(pieces[t].at[peer(*NEAR[k])], fulls[t].at[z * n8 + i8], ex_s.at[t, k], ex_r.at[t, k], near(*NEAR[k])))

    def from_peer(k):
        dx, dc = NEAR[k]
        return peer(RING - dx, dc)

    def wait_exchange(t, k):
        slot = fulls[t].at[z * n8 + from_peer(k)]
        copy(slot, slot, ex_s.at[t, k], ex_r.at[t, k], {"datb": z}).wait_recv()

    def z_first(t, k):
        src = pieces[t].at[i8] if k == 0 else fulls[t].at[z * n8 + from_peer(k)]
        dst = fulls[t].at[z * n8 + from_peer(k)]
        for side, step in enumerate((1, 3)):
            go(copy(src, dst, z1_s.at[t, side, k], z1_r.at[t, side, k], zdev(step)))

    def wait_z_first(t, side, k):
        back = 3 if side == 0 else 1
        slot = fulls[t].at[lax.rem(z + back, RING) * n8 + from_peer(k)]
        copy(slot, slot, z1_s.at[t, side, k], z1_r.at[t, side, k], {"datb": z}).wait_recv()

    def z_second(t):
        for k in range(n8 // 2):
            for side, step in enumerate((1, 3)):
                kk = k + side * (n8 // 2)
                wait_z_first(t, side, kk)
                back = 3 if side == 0 else 1
                slot = fulls[t].at[lax.rem(z + back, RING) * n8 + from_peer(kk)]
                go(copy(slot, slot, z2_s.at[t, side, k], z2_r.at[t, side, k], zdev(step)))

    def axes(r):
        return (ydev, xdev) if r == 0 else (xdev, ydev)

    def block(r, da, db, lo=0, size=rows):
        return row_block(x + db, y + da, lo, size) if r == 0 else row_block(x + da, y + db, lo, size)

    def to_core(r, ia, ib):
        own, full = rings[r]
        rb = block(r, DELTAS[ia], DELTAS[ib])
        src = own if ia == 0 and ib == 0 else full.at[rb]
        go(copy(src, full.at[rb], cc_s.at[r, ia, ib], cc_r.at[r, ia, ib], near(0, 1)))

    def first_own(r):
        own, full = rings[r]
        for side, step in enumerate((1, 3)):
            go(copy(own, full.at[block(r, 0, 0)], p1_s.at[r, side], p1_r.at[r, side], axes(r)[0](step)))

    def first_forward(r):
        own, full = rings[r]
        for side, step in enumerate((1, 3)):
            back = 3 if side == 0 else 1
            rb = full.at[block(r, back, 0)]
            copy(rb, rb, p1_s.at[r, side], p1_r.at[r, side], {"datb": z}).wait_recv()
            hb = full.at[block(r, back, 0, side * half, half)]
            go(copy(hb, hb, p2_s.at[r, side], p2_r.at[r, side], axes(r)[0](step)))

    def first_wait_far(r):
        own, full = rings[r]
        for side in range(2):
            hb = full.at[block(r, 2, 0, side * half, half)]
            copy(hb, hb, p2_s.at[r, side], p2_r.at[r, side], {"datb": z}).wait_recv()

    def second_send(r, ia):
        own, full = rings[r]
        rb = full.at[block(r, DELTAS[ia], 0)]
        src = own if ia == 0 else rb
        for side, step in enumerate((1, 3)):
            go(copy(src, rb, q1_s.at[r, side, ia], q1_r.at[r, side, ia], axes(r)[1](step)))

    def second_forward(r):
        own, full = rings[r]
        for ia in range(RING):
            for side, step in enumerate((1, 3)):
                back = 3 if side == 0 else 1
                rb = full.at[block(r, DELTAS[ia], back)]
                copy(rb, rb, q1_s.at[r, side, ia], q1_r.at[r, side, ia], {"datb": z}).wait_recv()
                if ia // 2 == side:
                    go(copy(rb, rb, q2_s.at[r, ia], q2_r.at[r, ia], axes(r)[1](step)))
                to_core(r, ia, 1 if side == 0 else 2)

    def second_wait_far(r):
        own, full = rings[r]
        for ia in range(RING):
            rb = full.at[block(r, DELTAS[ia], 2)]
            copy(rb, rb, q2_s.at[r, ia], q2_r.at[r, ia], {"datb": z}).wait_recv()
            to_core(r, ia, 3)

    exchange(0)
    z_first(0, 0)
    first_own(0)
    first_own(1)
    second_send(0, 0)
    second_send(1, 0)
    exchange(1)
    z_first(1, 0)
    exchange(2)
    z_first(2, 0)
    to_core(0, 0, 0)
    to_core(1, 0, 0)
    for k in range(1, n8):
        wait_exchange(0, k)
        z_first(0, k)
    for r in range(2):
        first_forward(r)
        for ia in (1, 2):
            second_send(r, ia)
            to_core(r, ia, 0)
    for k in range(1, n8):
        wait_exchange(1, k)
        z_first(1, k)
    for r in range(2):
        first_wait_far(r)
        second_send(r, 3)
        to_core(r, 3, 0)
    z_second(0)
    for k in range(1, n8):
        wait_exchange(2, k)
        z_first(2, k)
    for r in range(2):
        second_forward(r)
    z_second(1)
    for r in range(2):
        second_wait_far(r)
    z_second(2)

    for c in local:
        c.wait()
    for t in range(3):
        for k in range(n8 // 2):
            wait_z_first(t, 0, n8 // 2 + k)
            wait_z_first(t, 1, k)
            for side in range(2):
                slot = fulls[t].at[lax.rem(z + 2, RING) * n8 + from_peer(k + side * (n8 // 2))]
                copy(slot, slot, z2_s.at[t, side, k], z2_r.at[t, side, k], {"datb": z}).wait_recv()
    for r in range(2):
        own, full = rings[r]
        for ia in range(RING):
            for ib in range(RING):
                rb = full.at[other_core_rows(r, x, y, core, DELTAS[ia], DELTAS[ib], rows, half)]
                copy(rb, rb, cc_s.at[r, ia, ib], cc_r.at[r, ia, ib], {"datb": z}).wait_recv()
    for c in started:
        c.wait_send()


def other_core_rows(r, x, y, core, da, db, rows, half):
    px, py = (x + db, y + da) if r == 0 else (x + da, y + db)
    start = (lax.rem(px, RING) * 2 + 1 - core) * RING + lax.rem(py, RING)
    return pl.ds(pl.multiple_of(start * rows, half), rows)


def gather_all(pg, pu, pd, tok, grad):
    n8, dp, f8 = pg.shape
    rows, d = tok.shape
    hbm = pl.BlockSpec(memory_space=pl.ANY)
    dma = pltpu.SemaphoreType.DMA
    return pl.pallas_call(
        gather_kernel,
        out_shape=[jax.ShapeDtypeStruct((RING * n8, dp, f8), BF16)] * 3 + [jax.ShapeDtypeStruct((rows * RING * n8, d), BF16)] * 2,
        in_specs=[hbm] * 5,
        out_specs=[hbm] * 5,
        scratch_shapes=[
            dma((5,)),
            dma((3, n8)), dma((3, n8)),
            dma((3, 2, n8)), dma((3, 2, n8)),
            dma((3, 2, n8 // 2)), dma((3, 2, n8 // 2)),
            dma((2, 2)), dma((2, 2)),
            dma((2, 2)), dma((2, 2)),
            dma((2, 2, RING)), dma((2, 2, RING)),
            dma((2, RING)), dma((2, RING)),
            dma((2, RING, RING)), dma((2, RING, RING)),
        ],
        compiler_params=pltpu.CompilerParams(collective_id=0, has_side_effects=True),
        name="gather_all",
    )(pg, pu, pd, tok, grad)


LANE = 128
TAIL = (((0, 128), (384, 512)), ((128, 256), (512, 592)), ((256, 296), (296, 384)))
TAIL_TILES = ((0, 3), (1, 4), (2,))
OUT_COLS = 512


def reduce_kernel(f_ref, h_ref, wg, wu, wd, tok, grad, tok_own, grad_own,
                  og, ou, od, out, gin, ra, rb, give, rc, part, ra1, rb1, sd1, mid, ra2, rb2, sd2,
                  ff, blk, far, nxt, tmp, stage,
                  ff_sem, blk_sem, tmp_sem, a_s, a_r, f_s, f_r, d_s, d_r, e_s, e_r, own_sem,
                  c_s, c_r, a1_s, a1_r, f1_s, f1_r, d1_s, d1_r, a2_s, a2_r, f2_s, f2_r, d2_s, d2_r):
    z, y = lax.axis_index("datb"), lax.axis_index("model")
    x, core = lax.axis_index("x"), lax.axis_index("core")
    i8 = 2 * x + core
    n8 = 2 * RING
    nf = ff.shape[1]
    half = nf // 2
    cols = blk.shape[2]
    dp = cols // n8
    outs = (og, ou, od)

    def zdev(k):
        return {"datb": lax.rem(z + k, RING)}

    def xdev(k):
        return {"x": lax.rem(x + k, RING)}

    def ydev(k):
        return {"model": lax.rem(y + k, RING)}

    def near(dx, dc):
        return {"x": lax.rem(x + dx, RING), "core": lax.rem(core + dc, 2)}

    def peer(dx, dc):
        return 2 * lax.rem(x + dx, RING) + lax.rem(core + dc, 2)

    def rcopy(src, dst, s, r, dev):
        return pltpu.make_async_remote_copy(src_ref=src, dst_ref=dst, send_sem=s, recv_sem=r, device_id=dev, device_id_type=MESH_ID)

    def start(copies):
        for c in copies:
            c.start()

    def received(copies):
        for c in copies:
            c.wait_recv()

    def sent(copies):
        for c in copies:
            c.wait_send()

    barrier = pltpu.get_barrier_semaphore()
    others = [zdev(1), zdev(3), ydev(1), ydev(3)] + [near(*n) for n in NEAR[1:]]
    for dev in others:
        pl.semaphore_signal(barrier, inc=1, device_id=dev, device_id_type=MESH_ID)

    def ff_load(t):
        return pltpu.make_async_copy(f_ref.at[t], ff.at[t], ff_sem.at[t])

    def blk_load(t, slot, k):
        src = tok if t < 2 else grad
        lanes = pl.ds(pl.multiple_of(lax.rem(z + k, RING) * cols, LANE), cols)
        return pltpu.make_async_copy(src.at[:, lanes], blk.at[slot], blk_sem.at[slot])

    def product(t, slot, dst):
        step = 2 * LANE

        def one(n, carry):
            lanes = pl.ds(pl.multiple_of(jnp.minimum(n * step, cols - step), LANE), step)
            dst[:nf, lanes] = jnp.dot(ff[t], blk[slot, :, lanes], preferred_element_type=F32)
            return carry

        lax.fori_loop(0, -(-cols // step), one, 0)

    lo, hi = pl.ds(0, half), pl.ds(half, half)

    def a_copies(t):
        return [rcopy(far.at[t, rows], ra.at[t, rows], a_s.at[t, s], a_r.at[t, s], zdev(k)) for s, rows, k in ((0, lo, 1), (1, hi, 3))]

    def f_copies(t):
        return [rcopy(nxt.at[t, s, rows], rb.at[t, s, rows], f_s.at[t, s], f_r.at[t, s], zdev(k)) for s, rows, k in ((0, hi, 1), (1, lo, 3))]

    def d_rows(t):
        if t < 2:
            return [(0, 0, 0, half), (1, 0, half, half)]
        rows = []
        for p, (u, v) in enumerate(TAIL):
            rows += [(0, p, u[0], u[1] - u[0]), (1, p, v[0], v[1] - v[0])]
        return rows

    def d_copies(t):
        cs = []
        for s, p, first, size in d_rows(t):
            rows = pl.ds(first, size)
            cs.append(rcopy(nxt.at[t, s, rows], rb.at[t, s, rows], d_s.at[t, s, p], d_r.at[t, s, p], zdev(1 if s == 0 else 3)))
        return cs

    def far_blocks():
        for t in range(3):
            ff_load(t).wait()
            if t != 1:
                blk_load(t, t // 2, 2).wait()
            product(t, t // 2, far.at[t])
            start(a_copies(t))

    def next_blocks(t):
        if t != 1:
            blk_load(t, 0, 1).start()
            blk_load(t, 1, 3).start()
        for s in range(2):
            if t != 1:
                blk_load(t, s, 1 + 2 * s).wait()
            product(t, s, nxt.at[t, s])
        start(f_copies(t))
        received(a_copies(t))
        cs = [pltpu.make_async_copy(ra.at[t, rows], tmp.at[s, rows], tmp_sem.at[s]) for s, rows in ((0, lo), (1, hi))]
        start(cs)
        for c, (s, rows) in zip(cs, ((0, lo), (1, hi))):
            c.wait()
            nxt[t, s, rows] += tmp[s, rows]
        start(d_copies(t))

    def own_blocks():
        blk_load(0, 0, 0).start()
        blk_load(2, 1, 0).start()
        for t in range(3):
            sent(a_copies(t))
            if t != 1:
                blk_load(t, t // 2, 0).wait()
            product(t, t // 2, far.at[t])

    def load_sums(t, first, size):
        cs = [pltpu.make_async_copy(rb.at[t, s, pl.ds(first, size)], tmp.at[s, pl.ds(first, size)], tmp_sem.at[s]) for s in range(2)]
        start(cs)
        for c in cs:
            c.wait()

    def turn(t, tile, slot):
        rows = pl.ds(pl.multiple_of(tile * LANE, LANE), LANE)
        total = far[t, rows] + tmp[0, rows] + tmp[1, rows]
        stage[slot, :, rows] = total.T

    def hand_out(t, slot, p, lanes):
        cs = []
        for k in range(1, n8):
            rows = pl.ds(pl.multiple_of(peer(*NEAR[k]) * dp, 8), dp)
            cs.append(rcopy(stage.at[slot, rows, lanes], outs[t].at[i8, :, lanes], e_s.at[t, p, k], e_r.at[t, p, k], near(*NEAR[k])))
        rows = pl.ds(pl.multiple_of(i8 * dp, 8), dp)
        return cs, pltpu.make_async_copy(stage.at[slot, rows, lanes], outs[t].at[i8, :, lanes], own_sem.at[t, p])

    def handed(pair):
        sent(pair[0])
        pair[1].wait()

    tiles = stage.shape[2] // LANE
    every = pl.ds(0, tiles * LANE)

    def finish(t):
        received(f_copies(t) + d_copies(t))
        load_sums(t, 0, nf)

        def one(i, carry):
            turn(t, i, t)
            return carry

        lax.fori_loop(0, tiles, one, 0)
        cs, mine = hand_out(t, t, 0, every)
        start(cs + [mine])

    def finish_last():
        handed(hand_out(0, 0, 0, every))
        received(f_copies(2))
        dcs = d_copies(2)
        for p, group in enumerate(TAIL_TILES):
            received(dcs[2 * p:2 * p + 2])
            for tile in group:
                load_sums(2, tile * LANE, min(LANE, nf - tile * LANE))
                turn(2, tile, 0)
                cs, mine = hand_out(2, 0, tile, pl.ds(tile * LANE, LANE))
                start(cs + [mine])

    d = tok.shape[1]
    half_rows = tok_own.shape[1]
    rows = 2 * half_rows
    blocks = d // min(OUT_COLS, d)
    width = d // blocks

    def row_products(r, keep):
        side = core if keep else 1 - core
        terms = ((2, wd),) if r == 0 else ((0, wg), (1, wu))
        specs, args = [], []
        for t, w in terms:
            specs += [pl.BlockSpec((1, RING, 1, RING * rows, nf), lambda j, t=t: (t, 0, side, 0, 0)), pl.BlockSpec((width, nf), lambda j: (j, 0))]
            args += [h_ref, w]
        wide = pl.BlockSpec((RING, RING, rows, width), lambda j: (0, 0, 0, j))
        if keep:
            specs.append(wide)
            args.append(rc.at[r])

        def body(*refs):
            total = None
            for i in range(len(terms)):
                h = refs[2 * i][...].reshape(RING * RING * rows, nf)
                prod = dot(h, refs[2 * i + 1][...], 1, 1)
                total = prod if total is None else total + prod
            if keep:
                total = total + refs[-2][...].astype(F32).reshape(total.shape)
            refs[-1][...] = total.astype(BF16).reshape(RING, RING, rows, width)

        pltpu.emit_pipeline(body, grid=(blocks,), in_specs=specs, out_specs=[wide])(*args, (part if keep else give).at[r])

    def core_copy(r):
        return rcopy(give.at[r], rc.at[r], c_s.at[r], c_r.at[r], near(0, 1))

    def level(r, n):
        first = r == 0 if n == 1 else r == 1
        dev = ydev if first else xdev
        here = y if first else x
        if n == 1:
            def piece(k, h):
                at = lax.rem(here + k, RING)
                return part.at[r, pl.ds(2 * h, 2), at] if r == 0 else part.at[r, at, pl.ds(2 * h, 2)]
            return dev, piece, ra1, rb1, sd1, (a1_s, a1_r, f1_s, f1_r, d1_s, d1_r), (1, rows)

        def piece(k, h):
            return mid.at[r, lax.rem(here + k, RING), pl.ds(h, 1)]
        return dev, piece, ra2, rb2, sd2, (a2_s, a2_r, f2_s, f2_r, d2_s, d2_r), (1, half_rows)

    def ring_a(r, n):
        dev, piece, rfar, _, _, sems, _ = level(r, n)
        return [rcopy(piece(2, s), rfar.at[r, s], sems[0].at[r, s], sems[1].at[r, s], dev(1 + 2 * s)) for s in range(2)]

    def ring_f(r, n):
        dev, piece, _, rnear, _, sems, _ = level(r, n)
        return [rcopy(piece(1 + 2 * s, 1 - s), rnear.at[r, s, 1 - s], sems[2].at[r, s], sems[3].at[r, s], dev(1 + 2 * s)) for s in range(2)]

    def ring_d(r, n):
        dev, _, _, rnear, dep, sems, _ = level(r, n)
        return [rcopy(dep.at[r, s], rnear.at[r, s, s], sems[4].at[r, s], sems[5].at[r, s], dev(1 + 2 * s)) for s in range(2)]

    def add(srcs, dst):
        n = dst.shape[0]
        specs = [pl.BlockSpec((1,) + tuple(ref.shape[1:]), lambda i, rank=len(ref.shape): (i,) + (0,) * (rank - 1)) for ref in [*srcs, dst]]

        def body(*refs):
            total = refs[0][...].astype(F32)
            for ref in refs[1:-1]:
                total = total + ref[...].astype(F32)
            refs[-1][...] = total.astype(BF16).reshape(refs[-1].shape)

        pltpu.emit_pipeline(body, grid=(n,), in_specs=specs[:-1], out_specs=specs[-1:])(*srcs, dst)

    def ring_first(r, n):
        start(ring_a(r, n) + ring_f(r, n))

    def ring_dependent(r, n):
        _, piece, rfar, _, dep, _, _ = level(r, n)
        received(ring_a(r, n))
        for s in range(2):
            add([piece(1 + 2 * s, s), rfar.at[r, s]], dep.at[r, s])
            ring_d(r, n)[s].start()

    def ring_last(r, n):
        _, piece, _, rnear, _, _, _ = level(r, n)
        received(ring_f(r, n) + ring_d(r, n))
        for h in range(2):
            if n == 1:
                add([piece(0, h), rnear.at[r, 0, h], rnear.at[r, 1, h]], mid.at[r, pl.ds(2 * h, 2)])
            else:
                own, res = ((tok_own, out), (grad_own, gin))[r]
                hs = pl.ds(h, 1)
                add([own.at[hs], piece(0, h), rnear.at[r, 0, h], rnear.at[r, 1, h]], res.at[hs])

    for t in range(3):
        ff_load(t).start()
    blk_load(0, 0, 2).start()
    blk_load(2, 1, 2).start()
    pl.semaphore_wait(barrier, len(others))

    far_blocks()
    for r in range(2):
        row_products(r, False)
        core_copy(r).start()
    next_blocks(0)
    core_copy(0).wait_recv()
    row_products(0, True)
    ring_first(0, 1)
    next_blocks(1)
    core_copy(1).wait_recv()
    row_products(1, True)
    ring_first(1, 1)
    next_blocks(2)
    own_blocks()
    ring_dependent(0, 1)
    ring_dependent(1, 1)
    ring_last(0, 1)
    ring_first(0, 2)
    finish(0)
    ring_last(1, 1)
    ring_first(1, 2)
    ring_dependent(0, 2)
    ring_dependent(1, 2)
    ring_last(0, 2)
    ring_last(1, 2)
    finish(1)
    finish_last()

    last = [hand_out(1, 1, 0, every)] + [hand_out(2, 0, tile, pl.ds(tile * LANE, LANE)) for tile in range(tiles)]
    for pair in last:
        handed(pair)
    for pair in [hand_out(0, 0, 0, every)] + last:
        received(pair[0])
    for t in range(3):
        sent(f_copies(t) + d_copies(t))
    for r in range(2):
        core_copy(r).wait_send()
        for n in (1, 2):
            sent(ring_a(r, n) + ring_f(r, n) + ring_d(r, n))


def backward_reduce(f_all, h_all, wg, wu, wd, tok, grad, tok_own, grad_own):
    _, nf, tokens = f_all.shape
    rows, d = tok_own.shape
    cols = d // RING
    n8 = 2 * RING
    padded = -(-nf // LANE) * LANE
    hbm = pl.BlockSpec(memory_space=pl.ANY)
    dma = pltpu.SemaphoreType.DMA
    sds = jax.ShapeDtypeStruct
    halves = (2, rows // 2, d)
    res = pl.pallas_call(
        reduce_kernel,
        out_shape=[sds((n8, cols // n8, padded), F32)] * 3 + [sds(halves, BF16)] * 2 + [
            sds((3, nf, cols), F32), sds((3, 2, nf, cols), F32),
            sds((2, RING, RING, rows, d), BF16), sds((2, RING, RING, rows, d), BF16), sds((2, RING, RING, rows, d), BF16),
            sds((2, 2, 2, rows, d), BF16), sds((2, 2, 2, 2, rows, d), BF16), sds((2, 2, 2, rows, d), BF16),
            sds((2, RING, 2, rows // 2, d), BF16),
            sds((2, 2, 1, rows // 2, d), BF16), sds((2, 2, 2, 1, rows // 2, d), BF16), sds((2, 2, 1, rows // 2, d), BF16),
        ],
        in_specs=[hbm] * 9,
        out_specs=[hbm] * 17,
        scratch_shapes=[
            pltpu.VMEM((3, nf, tokens), BF16),
            pltpu.VMEM((2, tokens, cols), BF16),
            pltpu.VMEM((3, padded, cols), F32),
            pltpu.VMEM((3, 2, nf, cols), F32),
            pltpu.VMEM((2, padded, cols), F32),
            pltpu.VMEM((2, cols, padded), F32),
            dma((3,)), dma((2,)), dma((2,)),
            dma((3, 2)), dma((3, 2)),
            dma((3, 2)), dma((3, 2)),
            dma((3, 2, 3)), dma((3, 2, 3)),
            dma((3, 5, n8)), dma((3, 5, n8)),
            dma((3, 5)),
            dma((2,)), dma((2,)),
        ] + [dma((2, 2))] * 12,
        compiler_params=pltpu.CompilerParams(collective_id=1, has_side_effects=True, vmem_limit_bytes=63 * 1024 * 1024),
        cost_estimate=pl.CostEstimate(flops=12 * nf * tokens * d, bytes_accessed=200_000_000, transcendentals=0),
        name="backward_reduce",
    )(f_all, h_all.reshape(3, RING, 2, RING * rows, nf), wg, wu, wd, tok, grad, tok_own.reshape(halves), grad_own.reshape(halves))
    return res[:3], res[3].reshape(rows, d), res[4].reshape(rows, d)


def solution(mesh):
    nz, ny, nd = mesh.shape["datb"], mesh.shape["model"], mesh.shape["data"]
    nx, nc = nd // 2, 2
    fine = Mesh(mesh.devices.reshape(nz, ny, nx, nc), ("datb", "model", "x", "core"))

    def local_step(tok_loc, wg_loc, wu_loc, wd_loc, grad_loc):
        def by_owner(w):
            return w.reshape(w.shape[0], nd, w.shape[1] // nd).transpose(1, 0, 2)

        full = gather_all(by_owner(wg_loc), by_owner(wu_loc), by_owner(wd_loc.T), tok_loc, grad_loc)
        wg, wu, wdt = (w.reshape(-1, w.shape[2]) for w in full[:3])
        tok, grad = full[3:]

        gate_t = dot(wg, tok, 0, 1).astype(BF16).astype(F32)
        up_t = dot(wu, tok, 0, 1).astype(BF16).astype(F32)
        gh_t = dot(wdt, grad, 0, 1).astype(BF16).astype(F32)
        sig = jax.nn.sigmoid(gate_t)
        silu = gate_t * sig
        hid_t = (silu * up_t).astype(BF16)
        dgate_t = (gh_t * up_t * sig * (1.0 + gate_t * (1.0 - sig))).astype(BF16)
        dup_t = (gh_t * silu).astype(BF16)

        f_all = jnp.stack([dgate_t, dup_t, hid_t])
        h_all = jnp.stack([dgate_t.T, dup_t.T, hid_t.T])
        sums, out, grad_in = backward_reduce(f_all, h_all, wg, wu, wdt, tok, grad, tok_loc, grad_loc)
        grad_gate, grad_up, grad_down_t = (s[:, :, :wg.shape[1]].transpose(1, 0, 2).reshape(s.shape[1], -1) for s in sums)
        grad_down = grad_down_t.T
        return out, grad_in, grad_gate, grad_up, grad_down

    return jax.shard_map(local_step, mesh=fine, in_specs=(ROW_SPEC, GATE_SPEC, GATE_SPEC, DOWN_SPEC, ROW_SPEC), out_specs=(ROW_SPEC, ROW_SPEC, GATE_SPEC, GATE_SPEC, DOWN_SPEC), check_vma=False)
```

profile of v0, /device:TPU:1, one launch (start us, length us, event | category | flops | bytes accessed | tf_op | source)
XLA Modules:
  0.0 516.0 jit_solution(7931404107506880600)
XLA Ops:
  0.6 0.0 copy-start.3
  0.6 0.0 copy-start.2
  0.7 2.7 reshape.56
  3.3 1.1 copy.25
  4.5 0.0 copy-done.2
  4.5 1.5 reshape.57
  6.0 0.0 copy-done.3
  6.0 1.5 reshape.58
  7.5 1.7 copy_bitcast_fusion
  9.2 151.3 %gather_all.1 = (bf16[32,112,592]{2,1,0:T(8,128)(2,1)}, bf16[32,112,592]{2,1,0:T(8,128)(2,1)}, bf16[32,112,592]{2,1,0:T(8,128)(2,1)}, bf16[2048,3584]{1,0:T(8,128)(2,1)}, bf16[2048,3584]{1,0:T(8,128)(2,1)}) custom-call(bf16[8,112,592]{2,1,0:T(8,128)(2,1)} %bitcast.94, bf16[8,112,592]{2,1,0:T(8,128)(2,1)} %get-tuple-element.33.pu, ...), custom_call_target="tpu_custom_call" | custom-call | tf_op jit(solution)/shard_map/gather_all/pallas_call | solution.py:238
  160.5 0.0 copy-start.6
  160.5 14.8 %convolution_convert_fusion.2 = bf16[592,2048]{1,0:T(8,128)(2,1)S(1)} fusion(bf16[3584,592]{1,0:T(8,128)(2,1)} %bitcast.105, bf16[2048,3584]{1,0:T(8,128)(2,1)} %get-tuple-element.16.grad), kind=kOutput, calls=%fused_computation.37 | convolution fusion | flops 8691810304 | bytes 21348352 | tf_op jit(solution)/shard_map/dot_general | solution.py:23
  175.3 0.0 copy-done.6
  175.3 0.0 copy-start
  175.3 14.5 %convolution_convert_fusion = bf16[592,2048]{1,0:T(8,128)(2,1)S(1)} fusion(bf16[3584,592]{1,0:T(8,128)(2,1)S(1)} %bitcast.102, bf16[2048,3584]{1,0:T(8,128)(2,1)} %get-tuple-element.18.tok), kind=kOutput, calls=%fused_computation.35 | convolution fusion | flops 8691810304 | bytes 21348352 | tf_op jit(solution)/shard_map/dot_general | solution.py:23
  189.9 0.0 copy-done
  189.9 0.0 copy-start.1
  189.9 19.5 %fusion.9 = (bf16[2048,592]{0,1:T(8,128)(2,1)}, bf16[2048,592]{0,1:T(8,128)(2,1)}, bf16[2048,592]{0,1:T(8,128)(2,1)}, bf16[592,2048]{1,0:T(8,128)(2,1)}) fusion(bf16[592,2048]{1,0:T(8,128)(2,1)S(1)} %convolution_convert_fusion.2, bf16[592,2048]{1,0:T(8,128)(2,1)S(1)} %convolution_convert_fusion, bf16[3584,592]{1,0:T(8,128)(2,1)} %bitcast.103, ...), kind=kOutput, calls=%fused_computation.20 | convolution fusion | flops 8713633792 | bytes 33472512 | tf_op jit(solution)/shard_map/dot_general | solution.py:23
  209.4 0.0 copy-done.1
  209.4 3.1 copy.16
  212.5 5.5 %fusion.26 = (bf16[1,592,2048]{2,1,0:T(8,128)(2,1)S(1)}, bf16[1,592,2048]{2,1,0:T(8,128)(2,1)S(1)}, bf16[1,592,2048]{2,1,0:T(8,128)(2,1)S(1)}) fusion(bf16[592,2048]{1,0:T(8,128)(2,1)} %copy-done.1, bf16[592,2048]{1,0:T(8,128)(2,1)} %get-tuple-element.31, bf16[592,2048]{1,0:T(8,128)(2,1)} %copy-done), kind=kLoop, calls=%fused_computation.40 | loop fusion | flops 21823488 | bytes 14548992 | tf_op jit(solution)/shard_map/stack | solution.py:644
  218.0 3.6 pad_maximum_fusion.1.f_ref
  221.6 4.4 copy.17
  226.0 4.4 copy.18
  230.4 6.4 %pad_maximum_fusion.h_ref = bf16[3,4,2,256,592]{4,3,2,1,0:T(8,128)(2,1)} fusion(bf16[1,4,2,256,592]{4,3,2,1,0:T(8,128)(2,1)} %bitcast.93, bf16[1,4,2,256,592]{4,3,2,1,0:T(8,128)(2,1)} %bitcast.92, bf16[1,4,2,256,592]{4,3,2,1,0:T(8,128)(2,1)S(1)} %bitcast.91), kind=kLoop, calls=%fused_computation.4 | loop fusion | flops 7274496 | bytes 14548992 | tf_op jit(solution)/shard_map/stack | solution.py:645
  236.8 264.4 %backward_reduce.1 = (f32[8,112,640]{2,1,0:T(8,128)}, f32[8,112,640]{2,1,0:T(8,128)}, f32[8,112,640]{2,1,0:T(8,128)}, bf16[2,32,3584]{2,1,0:T(8,128)(2,1)}, bf16...) custom-call(bf16[3,592,2048]{2,1,0:T(8,128)(2,1)} %pad_maximum_fusio, ...), custom_call_target="tpu_custom_call" | custom-call | flops 52143587328 | bytes 200000000 | tf_op jit(solution)/shard_map/backward_reduce/pallas_call | solution.py:589
  501.2 1.8 slice_bitcast_fusion.2
  503.0 0.7 copy.19
  503.8 1.7 reshape.66
  505.5 1.8 slice_bitcast_fusion.1
  507.3 0.7 copy.20
  508.0 1.7 reshape.67
  509.7 1.8 slice_bitcast_fusion
  511.5 0.0 copy-start.5
  511.5 0.0 copy-start.4
  511.6 0.7 copy.21
  512.3 1.7 reshape.68
  514.0 0.0 copy-done.5
  514.0 0.8 copy.28
  514.8 0.0 copy-done.4
  514.8 0.8 copy.29
Async XLA Ops:
  0.6 5.3 %copy-start.3 = (bf16[4736,112]{0,1:T(8,128)(2,1)S(1)}, bf16[4736,112]{0,1:T(8,128)(2,1)}, u32[]{:S(2)}) copy-start(bf16[4736,112]{0,1:T(8,128)(2,1)} %param.8) | copy-start | bytes 3182596
  0.6 3.8 copy-start.2
  160.5 14.8 %copy-start.6 = (bf16[32,112,592]{2,1,0:T(8,128)(2,1)S(1)}, bf16[32,112,592]{2,1,0:T(8,128)(2,1)}, u32[]{:S(2)}) copy-start(bf16[32,112,592]{2,1,0:T(8,128)(2,1)} %get-tuple-element.19) | copy-start | bytes 12730372
  175.3 14.5 %copy-start = (bf16[592,2048]{1,0:T(8,128)(2,1)}, bf16[592,2048]{1,0:T(8,128)(2,1)S(1)}, u32[]{:S(2)}) copy-start(bf16[592,2048]{1,0:T(8,128)(2,1)S(1)} %convolution_convert_fusion.2) | copy-start | bytes 7274500
  189.9 19.5 %copy-start.1 = (bf16[592,2048]{1,0:T(8,128)(2,1)}, bf16[592,2048]{1,0:T(8,128)(2,1)S(1)}, u32[]{:S(2)}) copy-start(bf16[592,2048]{1,0:T(8,128)(2,1)S(1)} %convolution_convert_fusion) | copy-start | bytes 7274500
  511.5 2.5 copy-start.5
  511.5 3.2 copy-start.4
where the time goes:
time: 525 us; the launch traced here: 516 us
  Pallas kernels  416 us (79%)
  matrix products  48.8 us (9%)
  local copies, waits for them, and re-layouts  34.6 us (7%)
  other arithmetic  15.6 us (3%)
    pallas_call x1, Pallas kernels, backward_reduce(): pl.pallas_call(reduce_kernel, out_shape=[sds((n8, cols // n8, padded), F3...  264 us
    pallas_call x1, Pallas kernels, gather_all(): pl.pallas_call(gather_kernel, out_shape=[jax.ShapeDtypeStruct((RING * n8,...  151 us
    dot_general x3, matrix products, dot(): lax.dot_general(a, b, (((ca,), (cb,)), ((), ())), preferred_element_type=...  48.8 us

commit v1 on v0

--- a/solution.py
+++ b/solution.py
@@ -17,20 +17,25 @@
 RING = 4
 NEAR = ((0, 0), (0, 1), (1, 0), (3, 0), (1, 1), (3, 1), (2, 0), (2, 1))
 DELTAS = (0, 3, 1, 2)
+CHUNK = 256
 
 
 def dot(a, b, ca, cb):
     return lax.dot_general(a, b, (((ca,), (cb,)), ((), ())), preferred_element_type=F32)
 
 
-def gather_kernel(pg, pu, pd, tok, grad, wg, wu, wd, tok_all, grad_all,
-                  own_sem, ex_s, ex_r, z1_s, z1_r, z2_s, z2_r, p1_s, p1_r, p2_s, p2_r, q1_s, q1_r, q2_s, q2_r, cc_s, cc_r):
+def forward_kernel(pg, pu, pd, tok, grad, wg, wu, wd, tok_all, grad_all, f_all, h_all,
+                   wv, rowbuf, av, bv, hst, fst,
+                   own_sem, ex_s, ex_r, z1_s, z1_r, z2_s, z2_r, p1_s, p1_r, p2_s, p2_r, q1_s, q1_r, q2_s, q2_r, cc_s, cc_r,
+                   wv_sem, row_sem, hst_sem, fst_sem):
     z, y = lax.axis_index("datb"), lax.axis_index("model")
     x, core = lax.axis_index("x"), lax.axis_index("core")
     i8 = 2 * x + core
     n8 = 2 * RING
-    rows = tok.shape[0]
+    rows, d = tok.shape
     half = rows // 2
+    dp, nf = pg.shape[1:]
+    tokens = tok_all.shape[0]
 
     def peer(dx, dc):
         return 2 * lax.rem(x + dx, RING) + lax.rem(core + dc, 2)
@@ -54,205 +59,311 @@
     others = [zdev(1), zdev(3), ydev(1), ydev(3)] + [near(*n) for n in NEAR[1:]]
     for dev in others:
         pl.semaphore_signal(barrier, inc=1, device_id=dev, device_id_type=MESH_ID)
-    pl.semaphore_wait(barrier, len(others))
 
     pieces, fulls = (pg, pu, pd), (wg, wu, wd)
     started = []
 
-    def go(c):
-        c.start()
-        started.append(c)
-        return c
-
-    local = []
-    for t in range(3):
-        local.append(pltpu.make_async_copy(pieces[t].at[i8], fulls[t].at[z * n8 + i8], own_sem.at[t]))
-    rings = ((tok, tok_all), (grad, grad_all))
-
-    def row_block(px, py, lo=0, size=rows):
-        start = (lax.rem(px, RING) * 2 + core) * RING + lax.rem(py, RING)
-        return pl.ds(pl.multiple_of(start * rows + lo, half), size)
-
-    for t, (own, full) in enumerate(rings):
-        local.append(pltpu.make_async_copy(own, full.at[row_block(x, y)], own_sem.at[3 + t]))
-    for c in local:
-        c.start()
-
-    def exchange(t):
-        for k in range(1, n8):
-            go(copy(pieces[t].at[peer(*NEAR[k])], fulls[t].at[z * n8 + i8], ex_s.at[t, k], ex_r.at[t, k], near(*NEAR[k])))
+    def go(make, *args):
+        make(*args).start()
+        started.append((make, args))
+
+    def slot(t, zz, j):
+        return fulls[t].at[pl.ds(pl.multiple_of((zz * n8 + j) * dp, 16), dp)]
 
     def from_peer(k):
         dx, dc = NEAR[k]
         return peer(RING - dx, dc)
 
-    def wait_exchange(t, k):
-        slot = fulls[t].at[z * n8 + from_peer(k)]
-        copy(slot, slot, ex_s.at[t, k], ex_r.at[t, k], {"datb": z}).wait_recv()
+    def back(side):
+        return 3 if side == 0 else 1
+
+    def ahead(side):
+        return 1 if side == 0 else 3
+
+    def exchange_copy(t, k):
+        return copy(pieces[t].at[peer(*NEAR[k])], slot(t, z, i8), ex_s.at[t, k], ex_r.at[t, k], near(*NEAR[k]))
+
+    def exchange(t):
+        for k in range(1, n8):
+            go(exchange_copy, t, k)
+
+    def z_first_copy(t, side, k):
+        here = slot(t, z, from_peer(k))
+        return copy(here if k else pieces[t].at[i8], here, z1_s.at[t, side, k], z1_r.at[t, side, k], zdev(ahead(side)))
 
     def z_first(t, k):
-        src = pieces[t].at[i8] if k == 0 else fulls[t].at[z * n8 + from_peer(k)]
-        dst = fulls[t].at[z * n8 + from_peer(k)]
-        for side, step in enumerate((1, 3)):
-            go(copy(src, dst, z1_s.at[t, side, k], z1_r.at[t, side, k], zdev(step)))
+        if k:
+            here = slot(t, z, from_peer(k))
+            copy(here, here, ex_s.at[t, k], ex_r.at[t, k], {"datb": z}).wait_recv()
+        for side in range(2):
+            go(z_first_copy, t, side, k)
 
     def wait_z_first(t, side, k):
-        back = 3 if side == 0 else 1
-        slot = fulls[t].at[lax.rem(z + back, RING) * n8 + from_peer(k)]
-        copy(slot, slot, z1_s.at[t, side, k], z1_r.at[t, side, k], {"datb": z}).wait_recv()
+        there = slot(t, lax.rem(z + back(side), RING), from_peer(k))
+        copy(there, there, z1_s.at[t, side, k], z1_r.at[t, side, k], {"datb": z}).wait_recv()
+
+    def z_second_copy(t, side, k):
+        there = slot(t, lax.rem(z + back(side), RING), from_peer(k + side * (n8 // 2)))
+        return copy(there, there, z2_s.at[t, side, k], z2_r.at[t, side, k], zdev(ahead(side)))
 
     def z_second(t):
         for k in range(n8 // 2):
-            for side, step in enumerate((1, 3)):
-                kk = k + side * (n8 // 2)
-                wait_z_first(t, side, kk)
-                back = 3 if side == 0 else 1
-                slot = fulls[t].at[lax.rem(z + back, RING) * n8 + from_peer(kk)]
-                go(copy(slot, slot, z2_s.at[t, side, k], z2_r.at[t, side, k], zdev(step)))
-
-    def axes(r):
-        return (ydev, xdev) if r == 0 else (xdev, ydev)
-
-    def block(r, da, db, lo=0, size=rows):
-        return row_block(x + db, y + da, lo, size) if r == 0 else row_block(x + da, y + db, lo, size)
-
-    def to_core(r, ia, ib):
-        own, full = rings[r]
-        rb = block(r, DELTAS[ia], DELTAS[ib])
-        src = own if ia == 0 and ib == 0 else full.at[rb]
-        go(copy(src, full.at[rb], cc_s.at[r, ia, ib], cc_r.at[r, ia, ib], near(0, 1)))
-
-    def first_own(r):
-        own, full = rings[r]
-        for side, step in enumerate((1, 3)):
-            go(copy(own, full.at[block(r, 0, 0)], p1_s.at[r, side], p1_r.at[r, side], axes(r)[0](step)))
-
-    def first_forward(r):
-        own, full = rings[r]
-        for side, step in enumerate((1, 3)):
-            back = 3 if side == 0 else 1
-            rb = full.at[block(r, back, 0)]
-            copy(rb, rb, p1_s.at[r, side], p1_r.at[r, side], {"datb": z}).wait_recv()
-            hb = full.at[block(r, back, 0, side * half, half)]
-            go(copy(hb, hb, p2_s.at[r, side], p2_r.at[r, side], axes(r)[0](step)))
-
-    def first_wait_far(r):
-        own, full = rings[r]
-        for side in range(2):
-            hb = full.at[block(r, 2, 0, side * half, half)]
-            copy(hb, hb, p2_s.at[r, side], p2_r.at[r, side], {"datb": z}).wait_recv()
-
-    def second_send(r, ia):
-        own, full = rings[r]
-        rb = full.at[block(r, DELTAS[ia], 0)]
-        src = own if ia == 0 else rb
-        for side, step in enumerate((1, 3)):
-            go(copy(src, rb, q1_s.at[r, side, ia], q1_r.at[r, side, ia], axes(r)[1](step)))
-
-    def second_forward(r):
-        own, full = rings[r]
-        for ia in range(RING):
-            for side, step in enumerate((1, 3)):
-                back = 3 if side == 0 else 1
-                rb = full.at[block(r, DELTAS[ia], back)]
-                copy(rb, rb, q1_s.at[r, side, ia], q1_r.at[r, side, ia], {"datb": z}).wait_recv()
-                if ia // 2 == side:
-                    go(copy(rb, rb, q2_s.at[r, ia], q2_r.at[r, ia], axes(r)[1](step)))
-                to_core(r, ia, 1 if side == 0 else 2)
-
-    def second_wait_far(r):
-        own, full = rings[r]
-        for ia in range(RING):
-            rb = full.at[block(r, DELTAS[ia], 2)]
-            copy(rb, rb, q2_s.at[r, ia], q2_r.at[r, ia], {"datb": z}).wait_recv()
-            to_core(r, ia, 3)
-
-    exchange(0)
-    z_first(0, 0)
-    first_own(0)
-    first_own(1)
-    second_send(0, 0)
-    second_send(1, 0)
-    exchange(1)
-    z_first(1, 0)
-    exchange(2)
-    z_first(2, 0)
-    to_core(0, 0, 0)
-    to_core(1, 0, 0)
-    for k in range(1, n8):
-        wait_exchange(0, k)
-        z_first(0, k)
-    for r in range(2):
-        first_forward(r)
-        for ia in (1, 2):
-            second_send(r, ia)
-            to_core(r, ia, 0)
-    for k in range(1, n8):
-        wait_exchange(1, k)
-        z_first(1, k)
-    for r in range(2):
-        first_wait_far(r)
-        second_send(r, 3)
-        to_core(r, 3, 0)
-    z_second(0)
-    for k in range(1, n8):
-        wait_exchange(2, k)
-        z_first(2, k)
-    for r in range(2):
-        second_forward(r)
-    z_second(1)
-    for r in range(2):
-        second_wait_far(r)
-    z_second(2)
-
-    for c in local:
-        c.wait()
-    for t in range(3):
+            for side in range(2):
+                wait_z_first(t, side, k + side * (n8 // 2))
+                go(z_second_copy, t, side, k)
+
+    def weights_in(t):
         for k in range(n8 // 2):
             wait_z_first(t, 0, n8 // 2 + k)
             wait_z_first(t, 1, k)
             for side in range(2):
-                slot = fulls[t].at[lax.rem(z + 2, RING) * n8 + from_peer(k + side * (n8 // 2))]
-                copy(slot, slot, z2_s.at[t, side, k], z2_r.at[t, side, k], {"datb": z}).wait_recv()
-    for r in range(2):
-        own, full = rings[r]
+                there = slot(t, lax.rem(z + 2, RING), from_peer(k + side * (n8 // 2)))
+                copy(there, there, z2_s.at[t, side, k], z2_r.at[t, side, k], {"datb": z}).wait_recv()
+
+    cut = d // 2
+    rings = ((tok, tok_all, pl.ds(0, d), True), (grad, grad_all, pl.ds(0, cut), True), (grad, grad_all, pl.ds(cut, d - cut), False))
+
+    def axis(r, n):
+        return xdev if rings[r][3] == (n == 1) else ydev
+
+    def block(r, da, db, flip=0, lo=0, size=rows):
+        px, py = (x + da, y + db) if rings[r][3] else (x + db, y + da)
+        c = 1 - core if flip else core
+        first = (lax.rem(px, RING) * 2 + c) * RING + lax.rem(py, RING)
+        return rings[r][1].at[pl.ds(pl.multiple_of(first * rows + lo, half), size), rings[r][2]]
+
+    def own_block(r):
+        return rings[r][0].at[:, rings[r][2]]
+
+    def to_core_copy(r, ia, ib):
+        there = block(r, DELTAS[ia], DELTAS[ib])
+        return copy(own_block(r) if ia == 0 and ib == 0 else there, there, cc_s.at[r, ia, ib], cc_r.at[r, ia, ib], near(0, 1))
+
+    def to_core(r, ia, ib):
+        go(to_core_copy, r, ia, ib)
+
+    def first_copy(r, side):
+        return copy(own_block(r), block(r, 0, 0), p1_s.at[r, side], p1_r.at[r, side], axis(r, 1)(ahead(side)))
+
+    def first_own(r):
+        for side in range(2):
+            go(first_copy, r, side)
+
+    def first_far_copy(r, side):
+        part = block(r, back(side), 0, 0, side * half, half)
+        return copy(part, part, p2_s.at[r, side], p2_r.at[r, side], axis(r, 1)(ahead(side)))
+
+    def first_forward(r):
+        for side in range(2):
+            there = block(r, back(side), 0)
+            copy(there, there, p1_s.at[r, side], p1_r.at[r, side], {"datb": z}).wait_recv()
+            go(first_far_copy, r, side)
+        for ia in (1, 2):
+            second_send(r, ia)
+            to_core(r, ia, 0)
+
+    def first_far(r):
+        for side in range(2):
+            part = block(r, 2, 0, 0, side * half, half)
+            copy(part, part, p2_s.at[r, side], p2_r.at[r, side], {"datb": z}).wait_recv()
+        second_send(r, 3)
+        to_core(r, 3, 0)
+
+    def second_copy(r, side, ia):
+        there = block(r, DELTAS[ia], 0)
+        return copy(there if ia else own_block(r), there, q1_s.at[r, side, ia], q1_r.at[r, side, ia], axis(r, 2)(ahead(side)))
+
+    def second_send(r, ia):
+        for side in range(2):
+            go(second_copy, r, side, ia)
+
+    def second_far_copy(r, ia):
+        side = ia // 2
+        there = block(r, DELTAS[ia], back(side))
+        return copy(there, there, q2_s.at[r, ia], q2_r.at[r, ia], axis(r, 2)(ahead(side)))
+
+    def second_forward(r, ia):
+        for side in range(2):
+            there = block(r, DELTAS[ia], back(side))
+            copy(there, there, q1_s.at[r, side, ia], q1_r.at[r, side, ia], {"datb": z}).wait_recv()
+            if ia // 2 == side:
+                go(second_far_copy, r, ia)
+            to_core(r, ia, 1 if side == 0 else 2)
+
+    def second_far(r, ia):
+        there = block(r, DELTAS[ia], 2)
+        copy(there, there, q2_s.at[r, ia], q2_r.at[r, ia], {"datb": z}).wait_recv()
+        to_core(r, ia, 3)
+
+    def rows_in(r):
         for ia in range(RING):
             for ib in range(RING):
-                rb = full.at[other_core_rows(r, x, y, core, DELTAS[ia], DELTAS[ib], rows, half)]
-                copy(rb, rb, cc_s.at[r, ia, ib], cc_r.at[r, ia, ib], {"datb": z}).wait_recv()
-    for c in started:
-        c.wait_send()
-
-
-def other_core_rows(r, x, y, core, da, db, rows, half):
-    px, py = (x + db, y + da) if r == 0 else (x + da, y + db)
-    start = (lax.rem(px, RING) * 2 + 1 - core) * RING + lax.rem(py, RING)
-    return pl.ds(pl.multiple_of(start * rows, half), rows)
-
-
-def gather_all(pg, pu, pd, tok, grad):
-    n8, dp, f8 = pg.shape
+                there = block(r, DELTAS[ia], DELTAS[ib], 1)
+                copy(there, there, cc_s.at[r, ia, ib], cc_r.at[r, ia, ib], {"datb": z}).wait_recv()
+
+    local = [pltpu.make_async_copy(pieces[t].at[i8], slot(t, z, i8), own_sem.at[t]) for t in range(3)]
+    local += [pltpu.make_async_copy(own_block(r), block(r, 0, 0), own_sem.at[3 + r]) for r in range(3)]
+
+    n_chunk = tokens // CHUNK
+
+    def w_load(t):
+        return pltpu.make_async_copy(fulls[t], wv.at[t], wv_sem.at[t])
+
+    def row_load(src, i, buf):
+        first = pl.ds(pl.multiple_of(i * CHUNK, CHUNK), CHUNK)
+        return pltpu.make_async_copy(src.at[first], rowbuf.at[buf], row_sem.at[buf])
+
+    def chunk_loop(src, work, between):
+        row_load(src, 0, 0).start()
+
+        def body(i, carry):
+            buf = lax.rem(i, 2)
+
+            @pl.when(i + 1 < n_chunk)
+            def _():
+                row_load(src, i + 1, 1 - buf).start()
+
+            for k, step in enumerate(between):
+                pl.when(i == k)(step)
+            row_load(src, i, buf).wait()
+            work(i, buf)
+            return carry
+
+        lax.fori_loop(0, n_chunk, body, 0)
+
+    def chunk_rows(i):
+        return pl.ds(pl.multiple_of(i * CHUNK, CHUNK), CHUNK)
+
+    def pre_work(i, buf):
+        rb = rowbuf[buf]
+        av[chunk_rows(i)] = jnp.dot(rb, wv[0], preferred_element_type=F32).astype(BF16)
+        bv[chunk_rows(i)] = jnp.dot(rb, wv[1], preferred_element_type=F32).astype(BF16)
+
+    def out_copies(i, buf):
+        cs = [pltpu.make_async_copy(hst.at[buf, j], h_all.at[j, chunk_rows(i)], hst_sem.at[buf, j]) for j in range(3)]
+        return cs + [pltpu.make_async_copy(fst.at[buf, j], f_all.at[j, :, chunk_rows(i)], fst_sem.at[buf, j]) for j in range(3)]
+
+    def post_work(i, buf):
+        g = jnp.dot(rowbuf[buf], wv[2], preferred_element_type=F32).astype(BF16).astype(F32)
+
+        @pl.when(i >= 2)
+        def _():
+            for c in out_copies(i - 2, buf):
+                c.wait()
+
+        a, b = av[chunk_rows(i)].astype(F32), bv[chunk_rows(i)].astype(F32)
+        sig = jax.nn.sigmoid(a)
+        silu = a * sig
+        da = g * b * sig * (1.0 + a * (1.0 - sig))
+        for j, v in enumerate((da, g * silu, silu * b)):
+            hst[buf, j] = v.astype(BF16)
+            fst[buf, j] = v.T.astype(BF16)
+        for c in out_copies(i, buf):
+            c.start()
+
+    pl.semaphore_wait(barrier, len(others))
+    exchange(0)
+    z_first(0, 0)
+    first_own(0)
+    second_send(0, 0)
+    first_own(2)
+    for c in local:
+        c.start()
+    exchange(1)
+    first_own(1)
+    exchange(2)
+    second_send(1, 0)
+    second_send(2, 0)
+    for r in range(3):
+        to_core(r, 0, 0)
+    for k in range(1, n8):
+        z_first(0, k)
+    second_forward(0, 0)
+    first_forward(0)
+    z_first(1, 0)
+    z_first(1, 1)
+    z_second(0)
+    first_far(0)
+    first_forward(2)
+    for k in range(2, n8):
+        z_first(1, k)
+    second_forward(0, 1)
+    second_forward(0, 2)
+    first_forward(1)
+    first_far(2)
+    second_forward(0, 3)
+    first_far(1)
+    z_first(2, 0)
+    z_first(2, 1)
+    z_second(1)
+    for k in range(2, n8):
+        z_first(2, k)
+    weights_in(0)
+    for c in local:
+        c.wait()
+    w_load(0).start()
+    for ia in range(RING):
+        second_far(0, ia)
+    weights_in(1)
+    w_load(1).start()
+    rows_in(0)
+    w_load(0).wait()
+    w_load(1).wait()
+
+    def forward_grad(ia):
+        second_forward(2, ia)
+        second_forward(1, ia)
+
+    chunk_loop(tok_all, pre_work, [functools.partial(forward_grad, ia) for ia in range(RING)] + [functools.partial(z_second, 2)])
+    for ia in range(RING):
+        second_far(2, ia)
+        second_far(1, ia)
+    weights_in(2)
+    w_load(2).start()
+    rows_in(1)
+    rows_in(2)
+    w_load(2).wait()
+    chunk_loop(grad_all, post_work, ())
+    for i in (n_chunk - 2, n_chunk - 1):
+        for c in out_copies(i, i % 2):
+            c.wait()
+    for make, args in started:
+        make(*args).wait_send()
+
+
+def forward_gather(pg, pu, pd, tok, grad):
+    n8, dp, nf = pg.shape
     rows, d = tok.shape
+    tokens = rows * RING * n8
     hbm = pl.BlockSpec(memory_space=pl.ANY)
     dma = pltpu.SemaphoreType.DMA
+    sds = jax.ShapeDtypeStruct
     return pl.pallas_call(
-        gather_kernel,
-        out_shape=[jax.ShapeDtypeStruct((RING * n8, dp, f8), BF16)] * 3 + [jax.ShapeDtypeStruct((rows * RING * n8, d), BF16)] * 2,
+        forward_kernel,
+        out_shape=[sds((d, nf), BF16)] * 3 + [sds((tokens, d), BF16)] * 2 + [sds((3, nf, tokens), BF16), sds((3, tokens, nf), BF16)],
         in_specs=[hbm] * 5,
-        out_specs=[hbm] * 5,
+        out_specs=[hbm] * 7,
         scratch_shapes=[
-            dma((5,)),
+            pltpu.VMEM((3, d, nf), BF16),
+            pltpu.VMEM((2, CHUNK, d), BF16),
+            pltpu.VMEM((tokens, nf), BF16),
+            pltpu.VMEM((tokens, nf), BF16),
+            pltpu.VMEM((2, 3, CHUNK, nf), BF16),
+            pltpu.VMEM((2, 3, nf, CHUNK), BF16),
+            dma((6,)),
             dma((3, n8)), dma((3, n8)),
             dma((3, 2, n8)), dma((3, 2, n8)),
             dma((3, 2, n8 // 2)), dma((3, 2, n8 // 2)),
-            dma((2, 2)), dma((2, 2)),
-            dma((2, 2)), dma((2, 2)),
-            dma((2, 2, RING)), dma((2, 2, RING)),
-            dma((2, RING)), dma((2, RING)),
-            dma((2, RING, RING)), dma((2, RING, RING)),
+            dma((3, 2)), dma((3, 2)),
+            dma((3, 2)), dma((3, 2)),
+            dma((3, 2, RING)), dma((3, 2, RING)),
+            dma((3, RING)), dma((3, RING)),
+            dma((3, RING, RING)), dma((3, RING, RING)),
+            dma((3,)), dma((2,)), dma((2, 3)), dma((2, 3)),
         ],
-        compiler_params=pltpu.CompilerParams(collective_id=0, has_side_effects=True),
-        name="gather_all",
+        compiler_params=pltpu.CompilerParams(collective_id=0, has_side_effects=True, vmem_limit_bytes=60 * 1024 * 1024),
+        cost_estimate=pl.CostEstimate(flops=6 * nf * tokens * d, bytes_accessed=100_000_000, transcendentals=0),
+        name="forward_gather",
     )(pg, pu, pd, tok, grad)
 
 
@@ -621,31 +732,15 @@
 
 def solution(mesh):
     nz, ny, nd = mesh.shape["datb"], mesh.shape["model"], mesh.shape["data"]
-    nx, nc = nd // 2, 2
-    fine = Mesh(mesh.devices.reshape(nz, ny, nx, nc), ("datb", "model", "x", "core"))
+    fine = Mesh(mesh.devices.reshape(nz, ny, nd // 2, 2), ("datb", "model", "x", "core"))
 
     def local_step(tok_loc, wg_loc, wu_loc, wd_loc, grad_loc):
         def by_owner(w):
             return w.reshape(w.shape[0], nd, w.shape[1] // nd).transpose(1, 0, 2)
 
-        full = gather_all(by_owner(wg_loc), by_owner(wu_loc), by_owner(wd_loc.T), tok_loc, grad_loc)
-        wg, wu, wdt = (w.reshape(-1, w.shape[2]) for w in full[:3])
-        tok, grad = full[3:]
-
-        gate_t = dot(wg, tok, 0, 1).astype(BF16).astype(F32)
-        up_t = dot(wu, tok, 0, 1).astype(BF16).astype(F32)
-        gh_t = dot(wdt, grad, 0, 1).astype(BF16).astype(F32)
-        sig = jax.nn.sigmoid(gate_t)
-        silu = gate_t * sig
-        hid_t = (silu * up_t).astype(BF16)
-        dgate_t = (gh_t * up_t * sig * (1.0 + gate_t * (1.0 - sig))).astype(BF16)
-        dup_t = (gh_t * silu).astype(BF16)
-
-        f_all = jnp.stack([dgate_t, dup_t, hid_t])
-        h_all = jnp.stack([dgate_t.T, dup_t.T, hid_t.T])
+        wg, wu, wdt, tok, grad, f_all, h_all = forward_gather(by_owner(wg_loc), by_owner(wu_loc), by_owner(wd_loc.T), tok_loc, grad_loc)
         sums, out, grad_in = backward_reduce(f_all, h_all, wg, wu, wdt, tok, grad, tok_loc, grad_loc)
         grad_gate, grad_up, grad_down_t = (s[:, :, :wg.shape[1]].transpose(1, 0, 2).reshape(s.shape[1], -1) for s in sums)
-        grad_down = grad_down_t.T
-        return out, grad_in, grad_gate, grad_up, grad_down
+        return out, grad_in, grad_gate, grad_up, grad_down_t.T
 
     return jax.shard_map(local_step, mesh=fine, in_specs=(ROW_SPEC, GATE_SPEC, GATE_SPEC, DOWN_SPEC, ROW_SPEC), out_specs=(ROW_SPEC, ROW_SPEC, GATE_SPEC, GATE_SPEC, DOWN_SPEC), check_vma=False)

time: 525 us -> 462 us (0.88); the launches traced: 516 us -> 460 us
  matrix products: 48.8 us -> 0 us
  Pallas kernels: 416 us -> 437 us
  other arithmetic: 15.6 us -> 0 us
  local copies, waits for them, and re-layouts: 34.6 us -> 22.7 us
    dot_general x3 -> x0, matrix products: 48.8 us -> none  [dot(): lax.dot_general(a, b, (((ca,), (cb,)), ((), ())), preferred_element_type=...]
    pallas_call x1, Pallas kernels: 151 us -> 171 us  [forward_gather(): pl.pallas_call(forward_kernel, out_shape=[sds((d, nf), BF16)] * 3 + [sds(...]
    another operation x3 -> x0, other arithmetic: 15.6 us -> none  [the longest x2 9.17 us: local_step(): f_all = jnp.stack([dgate_t, dup_t, hid_t])]
    convert_element_type x3 -> x0, local copies, waits for them, and re-layouts: 11.8 us -> none  [the longest x1 4.38 us: local_step(): hid_t = (silu * up_t).astype(BF16)]
where the time goes in v1:
time: 462 us; the launch traced here: 460 us
  Pallas kernels  437 us (95%)
  local copies, waits for them, and re-layouts  22.7 us (5%)
    pallas_call x1, Pallas kernels, backward_reduce(): pl.pallas_call(reduce_kernel, out_shape=[sds((n8, cols // n8, padded), F3...  265 us
    pallas_call x1, Pallas kernels, forward_gather(): pl.pallas_call(forward_kernel, out_shape=[sds((d, nf), BF16)] * 3 + [sds(...  171 us

profile of v1, /device:TPU:1, one launch (start us, length us, event | category | flops | bytes accessed | tf_op | source)
XLA Modules:
  0.0 460.1 jit_solution(13948421531711005173)
XLA Ops:
  0.6 0.0 copy-start
  0.6 2.6 reshape.43
  3.3 0.0 copy-start.1
  3.3 1.1 copy.19
  4.4 0.0 copy-done
  4.4 1.5 reshape.44
  5.9 0.0 copy-done.1
  5.9 1.5 reshape.45
  7.4 1.7 copy_bitcast_fusion
  9.1 171.5 %forward_gather.1 = (bf16[3584,592]{1,0:T(8,128)(2,1)}, bf16[3584,592]{1,0:T(8,128)(2,1)}, bf16[3584,592]{1,0:T(8,128)(2,1)}, bf16[2048,3584]{1,0:T(8,128)(2,1)}...) custom-call(bf16[8,112,592]{2,1,0:T(8,128)(2,1)} %bitcast.21, ...), custom_call_target="tpu_custom_call" | custom-call | flops 26071793664 | bytes 100000000 | tf_op jit(solution)/shard_map/forward_gather/pallas_call | solution.py:341
  180.6 265.1 %backward_reduce.1 = (f32[8,112,640]{2,1,0:T(8,128)}, f32[8,112,640]{2,1,0:T(8,128)}, f32[8,112,640]{2,1,0:T(8,128)}, bf16[2,32,3584]{2,1,0:T(8,128)(2,1)}, bf16...) custom-call(bf16[3,592,2048]{2,1,0:T(8,128)(2,1)} %get-tuple-element, ...), custom_call_target="tpu_custom_call" | custom-call | flops 52143587328 | bytes 200000000 | tf_op jit(solution)/shard_map/backward_reduce/pallas_call | solution.py:700
  445.7 1.8 slice_bitcast_fusion.2
  447.5 0.7 copy.13
  448.3 1.7 reshape.51
  450.0 1.8 slice_bitcast_fusion.1
  451.8 0.7 copy.14
  452.5 1.7 reshape.52
  454.2 1.8 slice_bitcast_fusion
  456.0 0.7 copy.15
  456.8 0.0 copy-start.3
  456.8 0.0 copy-start.2
  456.8 1.7 reshape.53
  458.5 0.0 copy-done.3
  458.5 0.8 copy.22
  459.3 0.0 copy-done.2
  459.3 0.8 copy.23
Async XLA Ops:
  0.6 3.8 copy-start
  3.3 2.7 copy-start.1
  456.8 1.7 copy-start.3
  456.8 2.5 copy-start.2

commit v2 on v1

v2 whole, which is shorter than its diff:
```python
import functools

import jax
import jax.numpy as jnp
from jax import lax
from jax.experimental import pallas as pl
from jax.experimental.pallas import tpu as pltpu
from jax.sharding import Mesh
from jax.sharding import PartitionSpec as P

ROW_SPEC = P(("datb", "x", "core", "model"), None)
GATE_SPEC = P(("datb", "x", "core"), "model")
DOWN_SPEC = P("model", ("datb", "x", "core"))
BF16 = jnp.bfloat16
F32 = jnp.float32
MESH_ID = pl.DeviceIdType.MESH
RING = 4
NEAR = ((0, 0), (0, 1), (1, 0), (3, 0), (1, 1), (3, 1), (2, 0), (2, 1))
DELTAS = (0, 3, 1, 2)
CHUNK = 256
EX, Z1, Z2, P1, P2, BL, Q1, Q2, WD = range(9)
GATHER_STEPS = (
    (Z1, 0, 0), (EX, 0, 1), (EX, 0, 2), (EX, 0, 3), (EX, 0, 4), (EX, 0, 5), (EX, 0, 6), (EX, 0, 7), (Z1, 1, 0), (BL, 0, 0), (Z1, 2, 0),
    (EX, 1, 1), (EX, 2, 1), (P1, 2, 0), (P1, 2, 1), (P1, 0, 0), (P1, 0, 1), (Z1, 0, 1), (Z1, 1, 1), (BL, 1, 0), (Z1, 2, 1), (Z2, 0, 0, 0),
    (Z1, 0, 2), (EX, 1, 2), (EX, 1, 3), (Q1, 0, 0, 0), (Q1, 0, 0, 1), (Z1, 0, 3), (EX, 1, 4), (EX, 1, 5), (Z2, 0, 0, 1), (P2, 2, 1),
    (EX, 1, 6), (EX, 1, 7), (P2, 2, 0), (Z1, 0, 4), (Q1, 1, 0, 0), (Q1, 1, 0, 1), (Z1, 0, 5), (EX, 2, 2), (EX, 2, 3), (Z1, 0, 6), (P2, 0, 0),
    (P2, 0, 1), (BL, 0, 1), (Z2, 0, 0, 2), (Z2, 0, 1, 0), (Q2, 0, 0), (EX, 2, 4), (EX, 2, 5), (Z2, 0, 0, 3), (Z2, 0, 1, 1), (EX, 2, 6),
    (EX, 2, 7), (Z1, 0, 7), (Z2, 0, 1, 2), (BL, 0, 2), (Z2, 1, 0, 0), (Q2, 1, 0), (Q1, 0, 1, 1), (P1, 1, 0), (P1, 1, 1), (Z2, 1, 0, 1),
    (Z1, 1, 2), (Z2, 0, 1, 3), (BL, 2, 1), (BL, 0, 3), (Z1, 1, 3), (Q1, 0, 2, 1), (Z1, 1, 4), (BL, 2, 2), (Z1, 1, 5), (WD, 0), (BL, 2, 0),
    (Q1, 0, 1, 0), (Z1, 1, 6), (Q1, 0, 2, 0), (Q1, 0, 3, 1), (Z1, 1, 7), (Z2, 1, 1, 0), (P2, 1, 0), (P2, 1, 1), (Z2, 1, 0, 2), (BL, 2, 3),
    (Z2, 1, 1, 1), (Q1, 2, 1, 1), (Z2, 1, 0, 3), (BL, 1, 1), (Z2, 1, 1, 2), (Q1, 2, 1, 0), (Q1, 2, 2, 0), (Q1, 2, 2, 1), (Q1, 0, 3, 0),
    (Q2, 0, 2), (Z2, 2, 0, 0), (Z2, 1, 1, 3), (BL, 1, 2), (Z2, 2, 0, 1), (Q1, 2, 0, 0), (Q1, 2, 0, 1), (Z1, 2, 2), (BL, 1, 3), (Z1, 2, 3),
    (Q2, 0, 1), (Q2, 0, 3), (Q1, 2, 3, 0), (Q1, 2, 3, 1), (Z1, 2, 4), (WD, 1),
)
CHUNK_STEPS = (
    (
        (Q2, 2, 1), (Q2, 2, 2), (Z1, 2, 5), (Q1, 1, 1, 0), (Q1, 1, 1, 1),
    ),
    (
        (Z1, 2, 6), (Q1, 1, 2, 0), (Q1, 1, 2, 1),
    ),
    (
        (Q2, 2, 0), (Q2, 2, 3), (Z2, 2, 1, 0), (Z2, 2, 0, 2), (Q1, 1, 3, 0), (Q1, 1, 3, 1), (Z1, 2, 7),
    ),
    (
        (Z2, 2, 1, 1), (Z2, 2, 1, 2), (Z2, 2, 0, 3),
    ),
    (
        (Q2, 1, 1), (Q2, 1, 2),
    ),
    (
        (Q2, 1, 3), (Z2, 2, 1, 3),
    ),
    (),
)
LATE_STEPS = (
    (WD, 2),
)


def dot(a, b, ca, cb):
    return lax.dot_general(a, b, (((ca,), (cb,)), ((), ())), preferred_element_type=F32)


def forward_kernel(sg, su, sd, tok, grad, wg, wu, wd, tok_all, grad_all, f_all, h_all,
                   shard, pieces, wv, rowbuf, av, bv, hst, fst,
                   own_sem, ex_s, ex_r, z1_s, z1_r, z2_s, z2_r, p1_s, p1_r, p2_s, p2_r, q1_s, q1_r, q2_s, q2_r, cc_s, cc_r,
                   sh_sem, wv_sem, row_sem, hst_sem, fst_sem):
    z, y = lax.axis_index("datb"), lax.axis_index("model")
    x, core = lax.axis_index("x"), lax.axis_index("core")
    i8 = 2 * x + core
    n8 = 2 * RING
    rows, d = tok.shape
    half = rows // 2
    dp, nf = pieces.shape[2:]
    tokens = tok_all.shape[0]

    def peer(dx, dc):
        return 2 * lax.rem(x + dx, RING) + lax.rem(core + dc, 2)

    def zdev(k):
        return {"datb": lax.rem(z + k, RING)}

    def near(dx, dc):
        return {"x": lax.rem(x + dx, RING), "core": lax.rem(core + dc, 2)}

    def xdev(k):
        return {"x": lax.rem(x + k, RING)}

    def ydev(k):
        return {"model": lax.rem(y + k, RING)}

    def copy(src, dst, s, r, dev):
        return pltpu.make_async_remote_copy(src_ref=src, dst_ref=dst, send_sem=s, recv_sem=r, device_id=dev, device_id_type=MESH_ID)

    barrier = pltpu.get_barrier_semaphore()
    others = [zdev(1), zdev(3), ydev(1), ydev(3)] + [near(*n) for n in NEAR[1:]]
    for dev in others:
        pl.semaphore_signal(barrier, inc=1, device_id=dev, device_id_type=MESH_ID)

    fulls = (wg, wu, wd)
    loads = [pltpu.make_async_copy(src, shard.at[t], sh_sem.at[t]) for t, src in enumerate((sg, su, sd))]
    for c in loads:
        c.start()

    def cut_pieces(t):
        loads[t].wait()
        for j in range(n8):
            pieces[t, j] = shard[t, :, j * nf:(j + 1) * nf]

    started = []

    def go(make, *args):
        make(*args).start()
        started.append((make, args))

    def slot(t, zz, j):
        return fulls[t].at[pl.ds(pl.multiple_of((zz * n8 + j) * dp, 16), dp)]

    def from_peer(k):
        dx, dc = NEAR[k]
        return peer(RING - dx, dc)

    def back(side):
        return 3 if side == 0 else 1

    def ahead(side):
        return 1 if side == 0 else 3

    def exchange_copy(t, k):
        return copy(pieces.at[t, peer(*NEAR[k])], slot(t, z, i8), ex_s.at[t, k], ex_r.at[t, k], near(*NEAR[k]))

    def exchange(t, k):
        go(exchange_copy, t, k)

    def z_first_copy(t, side, k):
        here = slot(t, z, from_peer(k))
        return copy(here if k else pieces.at[t, i8], here, z1_s.at[t, side, k], z1_r.at[t, side, k], zdev(ahead(side)))

    def z_first(t, k):
        if k:
            here = slot(t, z, from_peer(k))
            copy(here, here, ex_s.at[t, k], ex_r.at[t, k], {"datb": z}).wait_recv()
        for side in range(2):
            go(z_first_copy, t, side, k)

    def wait_z_first(t, side, k):
        there = slot(t, lax.rem(z + back(side), RING), from_peer(k))
        copy(there, there, z1_s.at[t, side, k], z1_r.at[t, side, k], {"datb": z}).wait_recv()

    def z_second_copy(t, side, k):
        there = slot(t, lax.rem(z + back(side), RING), from_peer(k + side * (n8 // 2)))
        return copy(there, there, z2_s.at[t, side, k], z2_r.at[t, side, k], zdev(ahead(side)))

    def z_second(t, side, k):
        wait_z_first(t, side, k + side * (n8 // 2))
        go(z_second_copy, t, side, k)

    def weights_done(t):
        local[t].wait()
        for k in range(n8 // 2):
            wait_z_first(t, 0, n8 // 2 + k)
            wait_z_first(t, 1, k)
            for side in range(2):
                there = slot(t, lax.rem(z + 2, RING), from_peer(k + side * (n8 // 2)))
                copy(there, there, z2_s.at[t, side, k], z2_r.at[t, side, k], {"datb": z}).wait_recv()
        w_load(t).start()

    cut = d // 2
    rings = ((tok, tok_all, pl.ds(0, d), True), (grad, grad_all, pl.ds(0, cut), True), (grad, grad_all, pl.ds(cut, d - cut), False))

    def axis(r, n):
        return xdev if rings[r][3] == (n == 1) else ydev

    def block(r, da, db, flip=0, lo=0, size=rows):
        px, py = (x + da, y + db) if rings[r][3] else (x + db, y + da)
        c = 1 - core if flip else core
        first = (lax.rem(px, RING) * 2 + c) * RING + lax.rem(py, RING)
        return rings[r][1].at[pl.ds(pl.multiple_of(first * rows + lo, half), size), rings[r][2]]

    def own_block(r):
        return rings[r][0].at[:, rings[r][2]]

    def to_core_copy(r, ia, ib):
        there = block(r, DELTAS[ia], DELTAS[ib])
        return copy(own_block(r) if ia == 0 and ib == 0 else there, there, cc_s.at[r, ia, ib], cc_r.at[r, ia, ib], near(0, 1))

    def to_core(r, ia, ib):
        go(to_core_copy, r, ia, ib)

    def first_copy(r, side):
        return copy(own_block(r), block(r, 0, 0), p1_s.at[r, side], p1_r.at[r, side], axis(r, 1)(ahead(side)))

    def first_own(r, side):
        go(first_copy, r, side)

    def first_far_copy(r, side):
        part = block(r, back(side), 0, 0, side * half, half)
        return copy(part, part, p2_s.at[r, side], p2_r.at[r, side], axis(r, 1)(ahead(side)))

    def first_forward(r, side):
        there = block(r, back(side), 0)
        copy(there, there, p1_s.at[r, side], p1_r.at[r, side], {"datb": z}).wait_recv()
        go(first_far_copy, r, side)

    def block_on(r, ia):
        for side in range(2 if ia == 3 else 0):
            part = block(r, 2, 0, 0, side * half, half)
            copy(part, part, p2_s.at[r, side], p2_r.at[r, side], {"datb": z}).wait_recv()
        for side in range(2):
            go(second_copy, r, side, ia)
        to_core(r, ia, 0)

    def second_copy(r, side, ia):
        there = block(r, DELTAS[ia], 0)
        return copy(there if ia else own_block(r), there, q1_s.at[r, side, ia], q1_r.at[r, side, ia], axis(r, 2)(ahead(side)))

    def second_far_copy(r, ia):
        side = ia // 2
        there = block(r, DELTAS[ia], back(side))
        return copy(there, there, q2_s.at[r, ia], q2_r.at[r, ia], axis(r, 2)(ahead(side)))

    def second_forward(r, ia, side):
        there = block(r, DELTAS[ia], back(side))
        copy(there, there, q1_s.at[r, side, ia], q1_r.at[r, side, ia], {"datb": z}).wait_recv()
        if ia // 2 == side:
            go(second_far_copy, r, ia)
        to_core(r, ia, 1 if side == 0 else 2)

    def second_far(r, ia):
        there = block(r, DELTAS[ia], 2)
        copy(there, there, q2_s.at[r, ia], q2_r.at[r, ia], {"datb": z}).wait_recv()
        to_core(r, ia, 3)

    def rows_in(r):
        for ia in range(RING):
            for ib in range(RING):
                there = block(r, DELTAS[ia], DELTAS[ib], 1)
                copy(there, there, cc_s.at[r, ia, ib], cc_r.at[r, ia, ib], {"datb": z}).wait_recv()

    local = [pltpu.make_async_copy(pieces.at[t, i8], slot(t, z, i8), own_sem.at[t]) for t in range(3)]
    local += [pltpu.make_async_copy(own_block(r), block(r, 0, 0), own_sem.at[3 + r]) for r in range(3)]

    n_chunk = tokens // CHUNK

    def w_load(t):
        return pltpu.make_async_copy(fulls[t], wv.at[t], wv_sem.at[t])

    def row_load(src, i, buf):
        first = pl.ds(pl.multiple_of(i * CHUNK, CHUNK), CHUNK)
        return pltpu.make_async_copy(src.at[first], rowbuf.at[buf], row_sem.at[buf])

    def chunk_loop(src, work, between):
        row_load(src, 0, 0).start()

        def body(i, carry):
            buf = lax.rem(i, 2)

            @pl.when(i + 1 < n_chunk)
            def _():
                row_load(src, i + 1, 1 - buf).start()

            for k, step in enumerate(between):
                pl.when(i == k)(step)
            row_load(src, i, buf).wait()
            work(i, buf)
            return carry

        lax.fori_loop(0, n_chunk, body, 0)

    def chunk_rows(i):
        return pl.ds(pl.multiple_of(i * CHUNK, CHUNK), CHUNK)

    def pre_work(i, buf):
        rb = rowbuf[buf]
        av[chunk_rows(i)] = jnp.dot(rb, wv[0], preferred_element_type=F32).astype(BF16)
        bv[chunk_rows(i)] = jnp.dot(rb, wv[1], preferred_element_type=F32).astype(BF16)

    def out_copies(i, buf):
        cs = [pltpu.make_async_copy(hst.at[buf, j], h_all.at[j, chunk_rows(i)], hst_sem.at[buf, j]) for j in range(3)]
        return cs + [pltpu.make_async_copy(fst.at[buf, j], f_all.at[j, :, chunk_rows(i)], fst_sem.at[buf, j]) for j in range(3)]

    def post_work(i, buf):
        g = jnp.dot(rowbuf[buf], wv[2], preferred_element_type=F32).astype(BF16).astype(F32)

        @pl.when(i >= 2)
        def _():
            for c in out_copies(i - 2, buf):
                c.wait()

        a, b = av[chunk_rows(i)].astype(F32), bv[chunk_rows(i)].astype(F32)
        sig = jax.nn.sigmoid(a)
        silu = a * sig
        da = g * b * sig * (1.0 + a * (1.0 - sig))
        for j, v in enumerate((da, g * silu, silu * b)):
            hst[buf, j] = v.astype(BF16)
            fst[buf, j] = v.T.astype(BF16)
        for c in out_copies(i, buf):
            c.start()

    steps = (exchange, z_first, z_second, first_own, first_forward, block_on, second_forward, second_far, weights_done)

    def run(group):
        for which, *args in group:
            steps[which](*args)

    with jax.named_scope("begin"):
        for t in range(3):
            cut_pieces(t)
        pl.semaphore_wait(barrier, len(others))
        for c in local:
            c.start()
    with jax.named_scope("gather"):
        run(GATHER_STEPS)
        local[3].wait()
        rows_in(0)
        w_load(0).wait()
        w_load(1).wait()
    with jax.named_scope("gate_up"):
        chunk_loop(tok_all, pre_work, [functools.partial(run, group) for group in CHUNK_STEPS])
    with jax.named_scope("late"):
        run(LATE_STEPS)
        for r in (1, 2):
            local[3 + r].wait()
            rows_in(r)
        w_load(2).wait()
    with jax.named_scope("down"):
        chunk_loop(grad_all, post_work, ())
        for i in (n_chunk - 2, n_chunk - 1):
            for c in out_copies(i, i % 2):
                c.wait()
    for make, args in started:
        make(*args).wait_send()


def forward_gather(sg, su, sd, tok, grad):
    n8 = 2 * RING
    dp, nf = sg.shape[0], sg.shape[1] // n8
    rows, d = tok.shape
    tokens = rows * RING * n8
    hbm = pl.BlockSpec(memory_space=pl.ANY)
    dma = pltpu.SemaphoreType.DMA
    sds = jax.ShapeDtypeStruct
    return pl.pallas_call(
        forward_kernel,
        out_shape=[sds((d, nf), BF16)] * 3 + [sds((tokens, d), BF16)] * 2 + [sds((3, nf, tokens), BF16), sds((3, tokens, nf), BF16)],
        in_specs=[hbm] * 5,
        out_specs=[hbm] * 7,
        scratch_shapes=[
            pltpu.VMEM((3,) + sg.shape, BF16),
            pltpu.VMEM((3, n8, dp, nf), BF16),
            pltpu.VMEM((3, d, nf), BF16),
            pltpu.VMEM((2, CHUNK, d), BF16),
            pltpu.VMEM((tokens, nf), BF16),
            pltpu.VMEM((tokens, nf), BF16),
            pltpu.VMEM((2, 3, CHUNK, nf), BF16),
            pltpu.VMEM((2, 3, nf, CHUNK), BF16),
            dma((6,)),
            dma((3, n8)), dma((3, n8)),
            dma((3, 2, n8)), dma((3, 2, n8)),
            dma((3, 2, n8 // 2)), dma((3, 2, n8 // 2)),
            dma((3, 2)), dma((3, 2)),
            dma((3, 2)), dma((3, 2)),
            dma((3, 2, RING)), dma((3, 2, RING)),
            dma((3, RING)), dma((3, RING)),
            dma((3, RING, RING)), dma((3, RING, RING)),
            dma((3,)), dma((3,)), dma((2,)), dma((2, 3)), dma((2, 3)),
        ],
        compiler_params=pltpu.CompilerParams(collective_id=0, has_side_effects=True, vmem_limit_bytes=60 * 1024 * 1024),
        cost_estimate=pl.CostEstimate(flops=6 * nf * tokens * d, bytes_accessed=100_000_000, transcendentals=0),
        name="forward_gather",
    )(sg, su, sd, tok, grad)


LANE = 128
OUT_COLS = 512


def reduce_kernel(f_ref, h_ref, wg, wu, wd, tok, grad, tok_own, grad_own,
                  og, ou, od, out, gin, ra, rb, give, rc, part, ra1, rb1, sd1, mid, ra2, rb2, sd2,
                  ff, blk, far, nxt, tmp, stage,
                  ff_sem, blk_sem, tmp_sem, a_s, a_r, u_s, u_r, e_s, e_r, own_sem,
                  c_s, c_r, a1_s, a1_r, f1_s, f1_r, d1_s, d1_r, a2_s, a2_r, f2_s, f2_r, d2_s, d2_r):
    z, y = lax.axis_index("datb"), lax.axis_index("model")
    x, core = lax.axis_index("x"), lax.axis_index("core")
    i8 = 2 * x + core
    n8 = 2 * RING
    nf = ff.shape[1]
    half = nf // 2
    cols = blk.shape[2]
    dp = cols // n8
    outs = (og, ou, od)

    def zdev(k):
        return {"datb": lax.rem(z + k, RING)}

    def xdev(k):
        return {"x": lax.rem(x + k, RING)}

    def ydev(k):
        return {"model": lax.rem(y + k, RING)}

    def near(dx, dc):
        return {"x": lax.rem(x + dx, RING), "core": lax.rem(core + dc, 2)}

    def peer(dx, dc):
        return 2 * lax.rem(x + dx, RING) + lax.rem(core + dc, 2)

    def rcopy(src, dst, s, r, dev):
        return pltpu.make_async_remote_copy(src_ref=src, dst_ref=dst, send_sem=s, recv_sem=r, device_id=dev, device_id_type=MESH_ID)

    def start(copies):
        for c in copies:
            c.start()

    def received(copies):
        for c in copies:
            c.wait_recv()

    def sent(copies):
        for c in copies:
            c.wait_send()

    barrier = pltpu.get_barrier_semaphore()
    others = [zdev(1), zdev(3), ydev(1), ydev(3)] + [near(*n) for n in NEAR[1:]]
    for dev in others:
        pl.semaphore_signal(barrier, inc=1, device_id=dev, device_id_type=MESH_ID)

    def ff_load(t):
        return pltpu.make_async_copy(f_ref.at[t], ff.at[t], ff_sem.at[t])

    def blk_load(t, slot, k):
        src = tok if t < 2 else grad
        lanes = pl.ds(pl.multiple_of(lax.rem(z + k, RING) * cols, LANE), cols)
        return pltpu.make_async_copy(src.at[:, lanes], blk.at[slot], blk_sem.at[slot])

    def product(t, slot, dst):
        step = 2 * LANE

        def one(n, carry):
            lanes = pl.ds(pl.multiple_of(jnp.minimum(n * step, cols - step), LANE), step)
            dst[:nf, lanes] = jnp.dot(ff[t], blk[slot, :, lanes], preferred_element_type=F32)
            return carry

        lax.fori_loop(0, -(-cols // step), one, 0)

    lo, hi = pl.ds(0, half), pl.ds(half, half)

    def a_copies(t):
        return [rcopy(far.at[t, rows], ra.at[t, rows], a_s.at[t, s], a_r.at[t, s], zdev(k)) for s, rows, k in ((0, lo, 1), (1, hi, 3))]

    tiles = stage.shape[2] // LANE

    def tile_rows(tile):
        return pl.ds(tile * LANE, min(LANE, nf - tile * LANE))

    def unit_copies(t, tile):
        at = tile_rows(tile)
        return [rcopy(nxt.at[t, s, at], rb.at[t, s, at], u_s.at[t, s, tile], u_r.at[t, s, tile], zdev(1 + 2 * s)) for s in range(2)]

    def far_block(t):
        ff_load(t).wait()
        if t != 1:
            blk_load(t, t // 2, 2).wait()
        product(t, t // 2, far.at[t])
        start(a_copies(t))

    def next_blocks(t):
        for s in range(2):
            blk_load(t, s, 1 + 2 * s).start()
        for s in range(2):
            blk_load(t, s, 1 + 2 * s).wait()
            product(t, s, nxt.at[t, s])
        received(a_copies(t))
        cs = [pltpu.make_async_copy(ra.at[t, rows], tmp.at[s, rows], tmp_sem.at[s]) for s, rows in ((0, lo), (1, hi))]
        start(cs)
        for c, (s, rows) in zip(cs, ((0, lo), (1, hi))):
            c.wait()
            nxt[t, s, rows] += tmp[s, rows]
        for tile in range(tiles):
            start(unit_copies(t, tile))

    def own_block(t):
        blk_load(t, 0, 0).start()
        sent(a_copies(t))
        blk_load(t, 0, 0).wait()
        product(t, 0, far.at[t])

    def hand_out(t, tile):
        lanes = pl.ds(tile * LANE, LANE)
        cs = []
        for k in range(1, n8):
            at = pl.ds(pl.multiple_of(peer(*NEAR[k]) * dp, 8), dp)
            cs.append(rcopy(stage.at[t % 2, at, lanes], outs[t].at[i8, :, lanes], e_s.at[t, tile, k], e_r.at[t, tile, k], near(*NEAR[k])))
        at = pl.ds(pl.multiple_of(i8 * dp, 8), dp)
        return cs, pltpu.make_async_copy(stage.at[t % 2, at, lanes], outs[t].at[i8, :, lanes], own_sem.at[t, tile])

    def handed(t, tile):
        cs, mine = hand_out(t, tile)
        sent(cs)
        mine.wait()

    def finish(t, tile):
        received(unit_copies(t, tile))
        at = tile_rows(tile)
        cs = [pltpu.make_async_copy(rb.at[t, s, at], tmp.at[s, at], tmp_sem.at[s]) for s in range(2)]
        start(cs)
        if t == 2:
            handed(0, tile)
        for c in cs:
            c.wait()
        wide = pl.ds(tile * LANE, LANE)
        stage[t % 2, :, wide] = (far[t, wide] + tmp[0, wide] + tmp[1, wide]).T
        cs, mine = hand_out(t, tile)
        start(cs + [mine])

    d = tok.shape[1]
    half_rows = tok_own.shape[1]
    rows = 2 * half_rows
    blocks = d // min(OUT_COLS, d)
    width = d // blocks

    def row_products(r, keep):
        side = core if keep else 1 - core
        terms = ((2, wd),) if r == 0 else ((0, wg), (1, wu))
        specs, args = [], []
        for t, w in terms:
            specs += [pl.BlockSpec((1, RING, 1, RING * rows, nf), lambda j, t=t: (t, 0, side, 0, 0)), pl.BlockSpec((width, nf), lambda j: (j, 0))]
            args += [h_ref, w]
        wide = pl.BlockSpec((RING, RING, rows, width), lambda j: (0, 0, 0, j))
        if keep:
            specs.append(wide)
            args.append(rc.at[r])

        def body(*refs):
            total = None
            for i in range(len(terms)):
                h = refs[2 * i][...].reshape(RING * RING * rows, nf)
                prod = dot(h, refs[2 * i + 1][...], 1, 1)
                total = prod if total is None else total + prod
            if keep:
                total = total + refs[-2][...].astype(F32).reshape(total.shape)
            refs[-1][...] = total.astype(BF16).reshape(RING, RING, rows, width)

        pltpu.emit_pipeline(body, grid=(blocks,), in_specs=specs, out_specs=[wide])(*args, (part if keep else give).at[r])

    def core_copy(r):
        return rcopy(give.at[r], rc.at[r], c_s.at[r], c_r.at[r], near(0, 1))

    def level(n):
        if n == 1:
            def piece(r, k, h):
                return part.at[r, pl.ds(2 * h, 2), lax.rem(y + k, RING)]
            return ydev, piece, ra1, rb1, sd1, (a1_s, a1_r, f1_s, f1_r, d1_s, d1_r)

        def piece(r, k, h):
            return mid.at[r, lax.rem(x + k, RING), pl.ds(h, 1)]
        return xdev, piece, ra2, rb2, sd2, (a2_s, a2_r, f2_s, f2_r, d2_s, d2_r)

    def ring_a(r, n):
        dev, piece, rfar, _, _, sems = level(n)
        return [rcopy(piece(r, 2, s), rfar.at[r, s], sems[0].at[r, s], sems[1].at[r, s], dev(1 + 2 * s)) for s in range(2)]

    def ring_f(r, n):
        dev, piece, _, rnear, _, sems = level(n)
        return [rcopy(piece(r, 1 + 2 * s, 1 - s), rnear.at[r, s, 1 - s], sems[2].at[r, s], sems[3].at[r, s], dev(1 + 2 * s)) for s in range(2)]

    def ring_d(r, n):
        dev, _, _, rnear, dep, sems = level(n)
        return [rcopy(dep.at[r, s], rnear.at[r, s, s], sems[4].at[r, s], sems[5].at[r, s], dev(1 + 2 * s)) for s in range(2)]

    def add(srcs, dst):
        n = dst.shape[0]
        specs = [pl.BlockSpec((1,) + tuple(ref.shape[1:]), lambda i, rank=len(ref.shape): (i,) + (0,) * (rank - 1)) for ref in [*srcs, dst]]

        def body(*refs):
            total = refs[0][...].astype(F32)
            for ref in refs[1:-1]:
                total = total + ref[...].astype(F32)
            refs[-1][...] = total.astype(BF16).reshape(refs[-1].shape)

        pltpu.emit_pipeline(body, grid=(n,), in_specs=specs[:-1], out_specs=specs[-1:])(*srcs, dst)

    def ring_first(r, n):
        start(ring_a(r, n) + ring_f(r, n))

    def ring_dependent(r, n):
        _, piece, rfar, _, dep, _ = level(n)
        received(ring_a(r, n))
        for s in range(2):
            add([piece(r, 1 + 2 * s, s), rfar.at[r, s]], dep.at[r, s])
            ring_d(r, n)[s].start()

    def ring_last(r, n):
        _, piece, _, rnear, _, _ = level(n)
        received(ring_f(r, n) + ring_d(r, n))
        for h in range(2):
            if n == 1:
                add([piece(r, 0, h), rnear.at[r, 0, h], rnear.at[r, 1, h]], mid.at[r, pl.ds(2 * h, 2)])
            else:
                own, res = ((tok_own, out), (grad_own, gin))[r]
                hs = pl.ds(h, 1)
                add([own.at[hs], piece(r, 0, h), rnear.at[r, 0, h], rnear.at[r, 1, h]], res.at[hs])

    for t in range(3):
        ff_load(t).start()
    blk_load(0, 0, 2).start()
    blk_load(2, 1, 2).start()
    pl.semaphore_wait(barrier, len(others))

    def give_rows(r):
        row_products(r, False)
        core_copy(r).start()

    def keep_rows(r):
        core_copy(r).wait_recv()
        row_products(r, True)

    order = [
        (far_block, 0), (far_block, 1), (far_block, 2), (give_rows, 0), (give_rows, 1), (keep_rows, 0), (ring_first, 0, 1),
        (next_blocks, 0), (own_block, 0), (next_blocks, 1), (own_block, 1), (ring_dependent, 0, 1), (keep_rows, 1), (ring_first, 1, 1),
        (finish, 0, 0), (finish, 0, 1), (next_blocks, 2), (finish, 0, 2), (own_block, 2), (finish, 0, 3), (ring_last, 0, 1),
        (ring_first, 0, 2), (finish, 0, 4), (ring_dependent, 0, 2), (finish, 1, 0), (ring_dependent, 1, 1), (finish, 1, 1),
        (ring_last, 0, 2), (finish, 1, 2), (finish, 1, 3), (finish, 1, 4), (ring_last, 1, 1), (ring_first, 1, 2), (finish, 2, 0),
        (ring_dependent, 1, 2), (finish, 2, 1), (finish, 2, 2), (ring_last, 1, 2), (finish, 2, 3), (finish, 2, 4),
    ]
    for fn, *args in order:
        with jax.named_scope("_".join(str(v) for v in [fn.__name__, *args])):
            fn(*args)

    for t in range(3):
        for tile in range(tiles):
            sent(unit_copies(t, tile))
            received(hand_out(t, tile)[0])
            if t:
                handed(t, tile)
    for r in range(2):
        core_copy(r).wait_send()
        for n in (1, 2):
            sent(ring_a(r, n) + ring_f(r, n) + ring_d(r, n))


def backward_reduce(f_all, h_all, wg, wu, wd, tok, grad, tok_own, grad_own):
    _, nf, tokens = f_all.shape
    rows, d = tok_own.shape
    cols = d // RING
    n8 = 2 * RING
    tiles = -(-nf // LANE)
    padded = tiles * LANE
    hbm = pl.BlockSpec(memory_space=pl.ANY)
    dma = pltpu.SemaphoreType.DMA
    sds = jax.ShapeDtypeStruct
    halves = (2, rows // 2, d)
    res = pl.pallas_call(
        reduce_kernel,
        out_shape=[sds((n8, cols // n8, padded), F32)] * 3 + [sds(halves, BF16)] * 2 + [
            sds((3, nf, cols), F32), sds((3, 2, nf, cols), F32),
            sds((2, RING, RING, rows, d), BF16), sds((2, RING, RING, rows, d), BF16), sds((2, RING, RING, rows, d), BF16),
            sds((2, 2, 2, rows, d), BF16), sds((2, 2, 2, 2, rows, d), BF16), sds((2, 2, 2, rows, d), BF16),
            sds((2, RING, 2, rows // 2, d), BF16),
            sds((2, 2, 1, rows // 2, d), BF16), sds((2, 2, 2, 1, rows // 2, d), BF16), sds((2, 2, 1, rows // 2, d), BF16),
        ],
        in_specs=[hbm] * 9,
        out_specs=[hbm] * 17,
        scratch_shapes=[
            pltpu.VMEM((3, nf, tokens), BF16),
            pltpu.VMEM((2, tokens, cols), BF16),
            pltpu.VMEM((3, padded, cols), F32),
            pltpu.VMEM((3, 2, nf, cols), F32),
            pltpu.VMEM((2, padded, cols), F32),
            pltpu.VMEM((2, cols, padded), F32),
            dma((3,)), dma((2,)), dma((2,)),
            dma((3, 2)), dma((3, 2)),
            dma((3, 2, tiles)), dma((3, 2, tiles)),
            dma((3, tiles, n8)), dma((3, tiles, n8)),
            dma((3, tiles)),
            dma((2,)), dma((2,)),
        ] + [dma((2, 2))] * 12,
        compiler_params=pltpu.CompilerParams(collective_id=1, has_side_effects=True, vmem_limit_bytes=63 * 1024 * 1024),
        cost_estimate=pl.CostEstimate(flops=12 * nf * tokens * d, bytes_accessed=200_000_000, transcendentals=0),
        name="backward_reduce",
    )(f_all, h_all.reshape(3, RING, 2, RING * rows, nf), wg, wu, wd, tok, grad, tok_own.reshape(halves), grad_own.reshape(halves))
    return res[:3], res[3].reshape(rows, d), res[4].reshape(rows, d)


def assemble_kernel(og, ou, od, out, gin, g, u, w, res, gres, buf, flat, in_sem, out_sem, row_buf, row_sem):
    n8, nf = og.shape[0], g.shape[1] // og.shape[0]
    srcs, dsts = (og, ou, od), (g, u, w)
    rows_in = [pltpu.make_async_copy(src, row_buf.at[r], row_sem.at[r]) for r, src in enumerate((out, gin))]
    loads = [pltpu.make_async_copy(src, buf.at[t], in_sem.at[t]) for t, src in enumerate(srcs)]
    stores = [pltpu.make_async_copy(flat.at[t], dst, out_sem.at[t]) for t, dst in enumerate(dsts)]
    for c in loads + rows_in:
        c.start()
    for t in range(3):
        loads[t].wait()
        for j in range(n8):
            flat[t, :, j * nf:(j + 1) * nf] = buf[t, j, :, :nf]
        stores[t].start()
    rows_out = [pltpu.make_async_copy(row_buf.at[r], dst, row_sem.at[r]) for r, dst in enumerate((res, gres))]
    for c in rows_in:
        c.wait()
    for c in rows_out:
        c.start()
    for c in stores + rows_out:
        c.wait()


def assemble(sums, out, gin, ff):
    n8, dp, padded = sums[0].shape
    hbm = pl.BlockSpec(memory_space=pl.ANY)
    dma = pltpu.SemaphoreType.DMA
    sds = jax.ShapeDtypeStruct
    return pl.pallas_call(
        assemble_kernel,
        out_shape=[sds((dp, ff), F32)] * 3 + [sds(out.shape, BF16)] * 2,
        in_specs=[hbm] * 5,
        out_specs=[hbm] * 5,
        scratch_shapes=[
            pltpu.VMEM((3, n8, dp, padded), F32), pltpu.VMEM((3, dp, ff), F32), dma((3,)), dma((3,)),
            pltpu.VMEM((2,) + out.shape, BF16), dma((2,)),
        ],
        compiler_params=pltpu.CompilerParams(vmem_limit_bytes=63 * 1024 * 1024),
        name="assemble",
    )(*sums, out, gin)


def solution(mesh):
    nz, ny, nd = mesh.shape["datb"], mesh.shape["model"], mesh.shape["data"]
    fine = Mesh(mesh.devices.reshape(nz, ny, nd // 2, 2), ("datb", "model", "x", "core"))

    def local_step(tok_loc, wg_loc, wu_loc, wd_loc, grad_loc):
        wg, wu, wdt, tok, grad, f_all, h_all = forward_gather(wg_loc, wu_loc, wd_loc.T, tok_loc, grad_loc)
        sums, out, grad_in = backward_reduce(f_all, h_all, wg, wu, wdt, tok, grad, tok_loc, grad_loc)
        grad_gate, grad_up, grad_down_t, out, grad_in = assemble(sums, out, grad_in, wg_loc.shape[1])
        return out, grad_in, grad_gate, grad_up, grad_down_t.T

    return jax.shard_map(local_step, mesh=fine, in_specs=(ROW_SPEC, GATE_SPEC, GATE_SPEC, DOWN_SPEC, ROW_SPEC), out_specs=(ROW_SPEC, ROW_SPEC, GATE_SPEC, GATE_SPEC, DOWN_SPEC), check_vma=False)
```

time: 462 us -> 383 us (0.83)
  Pallas kernels: 437 us -> 379 us
  local copies, waits for them, and re-layouts: 22.7 us -> 0 us
    pallas_call x1, Pallas kernels: 265 us -> 228 us  [backward_reduce(): pl.pallas_call(reduce_kernel, out_shape=[sds((n8, cols // n8, padded), F3...]
    pallas_call x1, Pallas kernels: 171 us -> 146 us  [forward_gather(): pl.pallas_call(forward_kernel, out_shape=[sds((d, nf), BF16)] * 3 + [sds(...]
    reshape x7 -> x0, local copies, waits for them, and re-layouts: 11.9 us -> none  [the longest x4 6.76 us: by_owner(): return w.reshape(w.shape[0], nd, w.shape[1] // nd).transpose(1, 0, 2)]
    transpose x7 -> x0, local copies, waits for them, and re-layouts: 9.27 us -> none  [the longest x6 7.6 us: local_step(): s[:, :, :wg.shape[1]].transpose(1, 0, 2).reshape(s.shape[1], -1)]
    pallas_call x0 -> x1, Pallas kernels: none -> 5.37 us  [assemble(): pl.pallas_call(assemble_kernel, out_shape=[sds((dp, ff), F32)] * 3 + [sds...]
where the time goes in v2:
time: 383 us; the launch traced here: 380 us
  Pallas kernels  379 us (99%)
    pallas_call x1, Pallas kernels, backward_reduce(): pl.pallas_call(reduce_kernel, out_shape=[sds((n8, cols // n8, padded), F3...  228 us
    pallas_call x1, Pallas kernels, forward_gather(): pl.pallas_call(forward_kernel, out_shape=[sds((d, nf), BF16)] * 3 + [sds(...  146 us

profile of v2, /device:TPU:1, one launch (start us, length us, event | category | flops | bytes accessed | tf_op | source)
XLA Modules:
  0.0 380.2 jit_solution(18419141796535860442)
XLA Ops:
  0.6 146.1 %forward_gather.1 = (bf16[3584,592]{1,0:T(8,128)(2,1)}, bf16[3584,592]{1,0:T(8,128)(2,1)}, bf16[3584,592]{1,0:T(8,128)(2,1)}, bf16[2048,3584]{1,0:T(8,128)(2,1)}...) custom-call(bf16[112,4736]{1,0:T(8,128)(2,1)} %sg.1, ...), custom_call_target="tpu_custom_call" | custom-call | flops 26071793664 | bytes 100000000 | tf_op jit(solution)/shard_map/forward_gather/pallas_call | solution.py:344
  146.7 227.9 %backward_reduce.1 = (f32[8,112,640]{2,1,0:T(8,128)}, f32[8,112,640]{2,1,0:T(8,128)}, f32[8,112,640]{2,1,0:T(8,128)}, bf16[2,32,3584]{2,1,0:T(8,128)(2,1)}, bf16...) custom-call(bf16[3,592,2048]{2,1,0:T(8,128)(2,1)} %get-tuple-element, ...), custom_call_target="tpu_custom_call" | custom-call | flops 52143587328 | bytes 200000000 | tf_op jit(solution)/shard_map/backward_reduce/pallas_call | solution.py:654
  374.6 5.4 %assemble.1 = (f32[112,4736]{1,0:T(8,128)}, f32[112,4736]{1,0:T(8,128)}, f32[112,4736]{1,0:T(8,128)}, bf16[64,3584]{1,0:T(8,128)(2,1)}, bf16[64,3584]{1,0:T(8,128)(2,1)}) custom-call(f32[8,112,640]{2,1,0:T(8,128)} %get-tuple-element.29.og, f32[8,112,640]{2,1,0:T(8,128)} %get-tuple-element.30.ou, f32[8,112,640]{2,1,0:T(8,128)} %get-tuple-element.31.od, ...), custom_call_target="tpu_custom_call" | custom-call | tf_op jit(solution)/shard_map/assemble/pallas_call | solution.py:713
